TPU v7x, 8 devices: a whole 2x2x1 slice. The times are simulated.
8 devices in a mesh: data: 1 (over z), dap: 8 (over y, x, core).
Axes of the slice: x: 2, y: 2, z: 1, core: 2. Of those that a mesh axis runs over, the one named last changes fastest.
Arguments:
- msa_act: bfloat16 [256, 64, 64], P(('data', 'dap'))
- pair_act: bfloat16 [64, 64, 128], P(('data', 'dap'))
- msa_mask: int32 [256, 64], P('data')
- res_mask: int32 [64], P('data')
- w_row_bias: bfloat16 [2, 128, 8], replicated
- w_row_in: bfloat16 [2, 64, 4, 8, 8], replicated
- w_row_out: bfloat16 [2, 8, 8, 64], replicated
- w_col_in: bfloat16 [2, 64, 4, 8, 8], replicated
- w_col_out: bfloat16 [2, 8, 8, 64], replicated
- w_opm_in: bfloat16 [2, 64, 2, 32], replicated
- w_opm_out: bfloat16 [2, 32, 32, 128], replicated
- w_ts_bias: bfloat16 [2, 128, 4], replicated
- w_ts_in: bfloat16 [2, 128, 4, 4, 32], replicated
- w_ts_out: bfloat16 [2, 4, 32, 128], replicated
- w_te_bias: bfloat16 [2, 128, 4], replicated
- w_te_in: bfloat16 [2, 128, 4, 4, 32], replicated
- w_te_out: bfloat16 [2, 4, 32, 128], replicated
Outputs:
- output 1: bfloat16 [256, 64, 64], P(('data', 'dap'))
- output 2: bfloat16 [64, 64, 128], P(('data', 'dap'))
All inputs are finite; a program needn't handle non-finite values.
Results may differ from a plain program's by a relative error of at most 0.0187346.
Values are sent between devices in bfloat16 or wider.
A program may use at most 1 GiB of HBM per device.

v0:
```python
import functools

import jax
import jax.numpy as jnp
from jax import lax
from jax.experimental import pallas as pl
from jax.experimental.pallas import tpu as pltpu
from jax.sharding import PartitionSpec as P

F32 = jnp.float32
BF16 = jnp.bfloat16
LOG2E = 1.4426950408889634
NEG = -1e9
N = 8
R, W, S = 64, 128, 256

PH_RB1, PH_M1, PH_C1, PH_SB1, PH_Z1, PH_EB1, PH_RB2, PH_C2, PH_M2, PH_EB2, PH_Z2, PH_SB2 = range(12)


def mm(a, b):
    return jnp.dot(a, b, preferred_element_type=F32)


def mm_nt(a, b):
    return lax.dot_general(a, b, (((1,), (1,)), ((), ())), preferred_element_type=F32)


def iota(shape, dim):
    return lax.broadcasted_iota(jnp.int32, shape, dim)


def ln(x):
    mu = jnp.mean(x, axis=0, keepdims=True)
    c = x - mu
    var = jnp.mean(c * c, axis=0, keepdims=True)
    return (c * lax.rsqrt(var + 1e-5)).astype(BF16)


def rnd(x):
    return x.astype(BF16).astype(F32)


def low_lanes(rows):
    return iota((rows, W), 1) < R


def softmax_keys(x):
    e = jnp.exp2(x - jnp.max(x, axis=-2, keepdims=True))
    return (e * (1.0 / jnp.sum(e, axis=-2, keepdims=True))).astype(BF16)


def attend_pair(proj, heads, dim, bias_ref, key_mask, hm_ref, rm_ref):
    hd = heads * dim
    q, k, v, g = (proj[n * hd:(n + 1) * hd] for n in range(4))
    lo = low_lanes(hd)
    qbd = jnp.concatenate([jnp.where(lo, q, 0.0), jnp.where(lo, 0.0, q)], axis=0).astype(BF16)
    kt = jnp.transpose(k)
    kp = jnp.concatenate([kt[0:R], kt[R:W]], axis=1).astype(BF16)
    lhs = jnp.concatenate([kp] * heads, axis=0) * hm_ref[...]
    s = mm(lhs, qbd)
    x = s * (dim ** -0.5 * LOG2E) + bias_ref[...]
    x = jnp.where(key_mask[None] > 0, x.reshape(heads, R, W), NEG * LOG2E)
    p = softmax_keys(x).reshape(heads * R, W)
    vr = pltpu.roll(v, R, 1)
    v2 = jnp.concatenate([jnp.where(lo, v, vr), jnp.where(lo, vr, v)], axis=0).astype(BF16)
    vm = jnp.concatenate([v2] * (heads // 2), axis=1) * rm_ref[...]
    o2 = mm(vm, p)
    o = jnp.where(lo, o2[0:hd], o2[hd:2 * hd])
    return (o * jax.nn.sigmoid(g)).astype(BF16)


def kernel(axis, m_ref, z_ref, mt_ref, r_ref, wrb, wri, wro, wci, wco, woi, woo, wsb, wsi, wso, web, wei, weo, mo_ref, zo_ref,
           maskb, mp, mloc, rn, rkey, hm_r, rm_r, hm_t, rm_t, wro_t, wco_t, wso_t, weo_t, wall, wf,
           rowf, sm1, rm1, m1, sm2, rm2, aloc, remf, rem, cg, xop, zst, zf, sz, rz, pb,
           bm_r1, bm_r2, br_r1, br_r2, bm_s1, bm_s2, bm_e1, bm_e2, br_s1, br_s2, br_e1, br_e2, bt_r, bt_t, pq, send, recv):
    me = lax.axis_index(axis)
    peers = [lax.rem(me + k, N) for k in range(N)]
    senders = [lax.rem(me + N - k, N) for k in range(N)]

    def copy(ph, k, src, dst):
        return pltpu.make_async_remote_copy(
            src_ref=src, dst_ref=dst, send_sem=send.at[ph, k], recv_sem=recv.at[ph, k],
            device_id={axis: peers[k]}, device_id_type=pl.DeviceIdType.MESH)

    started = []

    def exchange(ph, src_of, dst_ref):
        for k in range(1, N):
            c = copy(ph, k, src_of(peers[k]), dst_ref.at[me])
            c.start()
            started.append(c)
        dst_ref[me] = src_of(me)[...]

    def arrive(ph, like, dst_ref):
        for k in range(1, N):
            copy(ph, k, like, dst_ref.at[senders[k]]).wait_recv()

    barrier = pltpu.get_barrier_semaphore()
    for k in range(1, N):
        pl.semaphore_signal(barrier, inc=1, device_id={axis: peers[k]}, device_id_type=pl.DeviceIdType.MESH)

    def bias_message(xln, w_bias, heads, msg):
        half = heads // 2
        b = mm(w_bias, xln)
        if heads == 4:
            b = jnp.concatenate([b, b], axis=0)
        bh = pltpu.roll(b, 8 - half, 0)
        lo = low_lanes(8)
        for i in range(8):
            bl_v = b[:, W * (i // 2):W * (i // 2) + W]
            bh_v = bh[:, W * (i // 2):W * (i // 2) + W]
            if i % 2 == 0:
                pb[8 * i:8 * i + 8, :] = jnp.where(lo, bl_v, pltpu.roll(bh_v, R, 1))
            else:
                pb[8 * i:8 * i + 8, :] = jnp.where(lo, pltpu.roll(bl_v, R, 1), bh_v)
        msg[...] = jnp.concatenate([pb[pl.ds(h, 8, stride=8), :] for h in range(half)], axis=0).astype(BF16)

    def bias_table(got, heads, table, gathered_keys):
        half = heads // 2
        full = got[...].astype(F32) * LOG2E
        for h in range(half):
            x = full[:, 8 * h:8 * h + 8, :].reshape(R, W)
            if gathered_keys:
                xr = pltpu.roll(x, R, 1)
                lo = low_lanes(R)
                table[R * h:R * h + R, :] = jnp.where(lo, x, xr)
                table[R * (half + h):R * (half + h) + R, :] = jnp.where(lo, xr, x)
            else:
                t = jnp.transpose(x)
                for hp in range(2):
                    blk = t[R * hp:R * hp + R]
                    table[R * (half * hp + h):R * (half * hp + h) + R, :] = jnp.concatenate([blk, blk], axis=1)

    def z_features():
        return jnp.concatenate(
            [jnp.transpose(zst[W * t:W * t + W, :].astype(F32)) for t in range(4)], axis=1)

    zst[...] = z_ref[...].reshape(512, W)
    bias_message(ln(z_features()), wrb[0], 8, bm_r1)
    pl.semaphore_wait(barrier, N - 1)
    exchange(PH_RB1, lambda p: bm_r1, br_r1)

    mt = mt_ref[...].astype(F32)
    mt_b = mt.astype(BF16)
    sel = (iota((S, W), 0) == 32 * me + iota((S, W), 1)) & (iota((S, W), 1) < 32)
    mloc[...] = mm(mt_b, jnp.where(sel, 1.0, 0.0).astype(BF16)).astype(BF16)
    mrows = mt_ref[pl.ds(pl.multiple_of(8 * me, 8), 8), :].astype(F32)
    t = iota((S, S), 1)
    perm = iota((S, S), 0) == (t % W) // 16 * 32 + t // W * 16 + t % 16
    mperm = mm(mrows.astype(BF16), jnp.where(perm, 1.0, 0.0).astype(BF16))
    mp[...] = mperm
    mpt = jnp.transpose(mperm)
    for i in range(8):
        maskb[i] = jnp.broadcast_to(mpt[:, i:i + 1], (S, W))
        row = jnp.broadcast_to(mrows[i:i + 1, :], (W, S)).astype(BF16)
        rn[i] = 1.0 / (1e-3 + mm_nt(mt_b, row))
    rkey[...] = jnp.transpose(jnp.broadcast_to(r_ref[...].astype(F32), (W, R)))

    def fill(ref, fn):
        ref[...] = jnp.where(fn(iota(ref.shape, 0), iota(ref.shape, 1)), 1.0, 0.0).astype(BF16)

    fill(hm_r, lambda r, c: r // R == (c % R) // 8)
    fill(rm_r, lambda r, c: (r % R) // 8 == c // R)
    fill(hm_t, lambda r, c: r // R == (c % W) // 32)
    fill(rm_t, lambda r, c: (r % W) // 32 == c // R)
    for b in range(2):
        wro_t[b] = jnp.transpose(wro[b].astype(F32)).astype(BF16)
        wco_t[b] = jnp.transpose(wco[b].astype(F32)).astype(BF16)
        wso_t[b] = jnp.transpose(wso[b].astype(F32)).astype(BF16)
        weo_t[b] = jnp.transpose(weo[b].astype(F32)).astype(BF16)
    wf[...] = woo[0].astype(F32)
    for n in range(32):
        a, b = n // 4, n % 4
        wall[0, 32 * a:32 * a + 32, W * b:W * b + W] = wf[pl.ds(n, 32, stride=32), :].astype(BF16)
        wall[1, 32 * a:32 * a + 32, W * b:W * b + W] = woo[1, 32 * n:32 * n + 32, :]

    def row_attention(b, xt, pair):
        proj = rnd(mm(wri[b], ln(xt)))
        r, c = iota((W, W), 0), iota((W, W), 1)
        pick = r == jnp.where(c < R, pair, pair + 16)
        key_mask = mm(mloc[...], jnp.where(pick, 1.0, 0.0).astype(BF16))
        gated = attend_pair(proj, 8, 8, bt_r, key_mask, hm_r, rm_r)
        return rnd(xt + mm(wro_t[b], gated))

    arrive(PH_RB1, bm_r1, br_r1)
    bias_table(br_r1, 8, bt_r, False)

    def row1(pair, carry):
        x = jnp.concatenate([m_ref[pair], m_ref[pair + 16]], axis=0).astype(F32)
        y = row_attention(0, jnp.transpose(x), pair)
        yt = jnp.transpose(y)
        rowf[pl.ds(pl.multiple_of(R * pair, R), R), :] = jnp.concatenate([yt[0:R], yt[R:W]], axis=1)
        return carry

    lax.fori_loop(0, 16, row1, 0)
    for i in range(R):
        sm1[i // 8, i % 8] = rowf[pl.ds(i, 16, stride=R), :].astype(BF16)
    exchange(PH_M1, lambda p: sm1.at[p], rm1)

    def column_attention(b, xt, i):
        proj = rnd(mm(wci[b], ln(xt)))
        q, k, v, g = (proj[R * n:R * n + R] for n in range(4))
        kt = jnp.transpose(k).astype(BF16)
        head = iota((R, S), 0) // 8
        key_mask = maskb[i] > 0
        out = []
        for h in range(8):
            s = mm(kt, jnp.where(head == h, q, 0.0).astype(BF16))
            vh = v[8 * h:8 * h + 8].astype(BF16)
            parts = []
            for n in range(2):
                x = jnp.where(key_mask, s[:, W * n:W * n + W] * (8 ** -0.5 * LOG2E), NEG * LOG2E)
                parts.append(softmax_keys(x))
            out.append(mm(vh, jnp.concatenate(parts, axis=1)))
        o = jnp.concatenate(out, axis=0)
        gated = (o * jax.nn.sigmoid(g)).astype(BF16)
        return rnd(xt + mm(wco_t[b], gated))

    def opm_operands(b, xt, i):
        proj = mm(woi[b], ln(xt)) * mp[pl.ds(i, 1), :]
        near, far = (proj[0:32], proj[32:R]) if b == 0 else (proj[32:R], proj[0:32])
        rows = pl.ds(pl.multiple_of(32 * i, 32), 32)
        aloc[b, rows, :] = near.astype(BF16)
        remf[0, rows, :] = far[:, 0:W]
        remf[1, rows, :] = far[:, W:S]

    def pack_far(b):
        for n in range(16):
            for t in range(2):
                rem[b, 16 * n:16 * n + 16, W * t:W * t + W] = jnp.concatenate(
                    [remf[t, pl.ds(2 * n + u, 8, stride=32), :] for u in range(2)], axis=0).astype(BF16)

    arrive(PH_M1, sm1.at[0], rm1)

    def col1(i, carry):
        x = rm1[:, i].reshape(W, W).astype(F32)
        xt = jnp.transpose(x)
        y = column_attention(0, jnp.concatenate([xt[0:R], xt[R:W]], axis=1), i)
        m1[i] = y.astype(BF16)
        opm_operands(0, y, i)
        return carry

    lax.fori_loop(0, 8, col1, 0)
    pack_far(0)
    exchange(PH_C1, lambda p: rem.at[0], cg.at[0])

    def col2(i, carry):
        y = column_attention(1, m1[i].astype(F32), i)
        opm_operands(1, y, i)
        yt = jnp.transpose(jnp.concatenate([y[:, 0:W], y[:, W:S]], axis=0)).astype(BF16)
        sm2[:, i] = yt.reshape(8, 16, W)
        return carry

    lax.fori_loop(0, 8, col2, 0)
    exchange(PH_M2, lambda p: sm2.at[p], rm2)
    pack_far(1)

    def opm(b):
        for n in range(8):
            far = cg[b, :, 32 * n:32 * n + 32, :].reshape(S, S)
            o = mm_nt(aloc[b], far).astype(BF16)
            for i in range(8):
                xop[i, 32 * n:32 * n + 32, :] = o[32 * i:32 * i + 32, :]

        def one(i, carry):
            y = mm(jnp.transpose(xop[i]), wall[b]).reshape(8, 4, 8, 512)
            u = sum(y[:, n, :, W * n:W * n + W] for n in range(4)).reshape(R, W)
            rows = pl.ds(pl.multiple_of(R * i, R), R)
            zst[rows, :] = (zst[rows, :].astype(F32) + u * rn[i]).astype(BF16)
            return carry

        lax.fori_loop(0, 8, one, 0)

    def tri_project(xln, w_in):
        pq[...] = rnd(mm(w_in, xln))

    def tri_attend(x, w_out_t):
        out = []
        for t in range(4):
            gated = attend_pair(pq[:, W * t:W * t + W], 4, 32, bt_t, rkey[...], hm_t, rm_t)
            out.append(rnd(x[:, W * t:W * t + W] + mm(w_out_t, gated)))
        return jnp.concatenate(out, axis=1)

    def swap_pair(y, n):
        for t in range(4):
            zf[W * t:W * t + W, :] = jnp.transpose(y[:, W * t:W * t + W])
        for c in range(32):
            sz[n, 16 * c:16 * c + 16, :] = jnp.concatenate(
                [zf[pl.ds(2 * c, 8, stride=R), :], zf[pl.ds(2 * c + 1, 8, stride=R), :]], axis=0).astype(BF16)

    def take_pair(n):
        x = rz[n].astype(F32).reshape(8, 8, 8, W)
        for j in range(8):
            zst[R * j:R * j + R, :] = x[:, j].reshape(R, W).astype(BF16)

    def z_block(n, p):
        return sz.at[n, pl.ds(pl.multiple_of(R * p, R), R), :]

    arrive(PH_C1, rem.at[0], cg.at[0])
    exchange(PH_C2, lambda p: rem.at[1], cg.at[1])
    opm(0)
    x = z_features()
    xln = ln(x)
    bias_message(xln, wsb[0], 4, bm_s1)
    exchange(PH_SB1, lambda p: bm_s1, br_s1)
    tri_project(xln, wsi[0])
    arrive(PH_SB1, bm_s1, br_s1)
    bias_table(br_s1, 4, bt_t, False)
    y = tri_attend(x, wso_t[0])
    swap_pair(y, 0)
    exchange(PH_Z1, lambda p: z_block(0, p), rz.at[0])
    bias_message(ln(y), web[0], 4, bm_e1)
    exchange(PH_EB1, lambda p: bm_e1, br_e1)
    arrive(PH_Z1, z_block(0, 0), rz.at[0])
    take_pair(0)
    x = z_features()
    tri_project(ln(x), wei[0])
    arrive(PH_EB1, bm_e1, br_e1)
    bias_table(br_e1, 4, bt_t, True)
    y = tri_attend(x, weo_t[0])
    bias_message(ln(y), wrb[1], 8, bm_r2)
    exchange(PH_RB2, lambda p: bm_r2, br_r2)
    for t in range(4):
        zst[W * t:W * t + W, :] = jnp.transpose(y[:, W * t:W * t + W]).astype(BF16)

    arrive(PH_C2, rem.at[1], cg.at[1])
    opm(1)
    x = z_features()
    xln = ln(x)
    bias_message(xln, web[1], 4, bm_e2)
    exchange(PH_EB2, lambda p: bm_e2, br_e2)
    tri_project(xln, wei[1])

    arrive(PH_M2, sm2.at[0], rm2)
    arrive(PH_RB2, bm_r2, br_r2)
    bias_table(br_r2, 8, bt_r, True)
    rowf[...] = rm2[...].reshape(1024, W).astype(F32)

    def row2(pair, carry):
        xt = jnp.transpose(rowf[pl.ds(pair, R, stride=16), :])
        xm = jnp.concatenate([xt[0:R], xt[R:W]], axis=1)
        yt = jnp.transpose(row_attention(1, xm, pair)).astype(BF16)
        mo_ref[pair] = yt[0:R]
        mo_ref[pair + 16] = yt[R:W]
        return carry

    lax.fori_loop(0, 16, row2, 0)

    arrive(PH_EB2, bm_e2, br_e2)
    bias_table(br_e2, 4, bt_t, False)
    y = tri_attend(x, weo_t[1])
    swap_pair(y, 1)
    exchange(PH_Z2, lambda p: z_block(1, p), rz.at[1])
    bias_message(ln(y), wsb[1], 4, bm_s2)
    exchange(PH_SB2, lambda p: bm_s2, br_s2)
    arrive(PH_Z2, z_block(1, 0), rz.at[1])
    take_pair(1)
    x = z_features()
    tri_project(ln(x), wsi[1])
    arrive(PH_SB2, bm_s2, br_s2)
    bias_table(br_s2, 4, bt_t, True)
    y = tri_attend(x, wso_t[1])
    for t in range(4):
        zo_ref[2 * t:2 * t + 2] = jnp.transpose(y[:, W * t:W * t + W]).astype(BF16).reshape(2, R, W)

    for c in started:
        c.wait_send()


def solution(mesh):
    axis = 'dap'

    def local_step(m, z, msa_mask, res_mask, w_row_bias, w_row_in, w_row_out, w_col_in, w_col_out, w_opm_in, w_opm_out,
                   w_ts_bias, w_ts_in, w_ts_out, w_te_bias, w_te_in, w_te_out):
        def tin(w):
            return jnp.moveaxis(w, 1, -1).reshape(2, -1, w.shape[1])

        args = (m, z, msa_mask.T, res_mask[None, :],
                tin(w_row_bias), tin(w_row_in), w_row_out.reshape(2, R, R), tin(w_col_in), w_col_out.reshape(2, R, R),
                tin(w_opm_in), w_opm_out.reshape(2, 1024, W),
                tin(w_ts_bias), tin(w_ts_in), w_ts_out.reshape(2, W, W),
                tin(w_te_bias), tin(w_te_in), w_te_out.reshape(2, W, W))
        v = pltpu.VMEM
        scratch = [
            v((8, S, W), F32), v((8, S), F32), v((R, W), BF16), v((8, R, W), F32), v((R, W), F32),
            v((512, W), BF16), v((W, 512), BF16), v((S, S), BF16), v((S, S), BF16),
            v((2, R, R), BF16), v((2, R, R), BF16), v((2, W, W), BF16), v((2, W, W), BF16),
            v((2, S, 512), BF16), v((1024, W), F32),
            v((1024, W), F32), v((8, 8, 16, W), BF16), v((8, 8, 16, W), BF16), v((8, R, S), BF16),
            v((8, 8, 16, W), BF16), v((8, 8, 16, W), BF16),
            v((2, S, S), BF16), v((2, S, W), F32), v((2, S, S), BF16), v((2, 8, S, S), BF16), v((8, S, S), BF16),
            v((512, W), BF16), v((512, W), F32), v((2, 512, W), BF16), v((2, 8, R, W), BF16), v((R, W), F32),
            v((32, W), BF16), v((32, W), BF16), v((8, 32, W), BF16), v((8, 32, W), BF16),
            v((16, W), BF16), v((16, W), BF16), v((16, W), BF16), v((16, W), BF16),
            v((8, 16, W), BF16), v((8, 16, W), BF16), v((8, 16, W), BF16), v((8, 16, W), BF16),
            v((512, W), F32), v((S, W), F32), v((512, 512), F32),
            pltpu.SemaphoreType.DMA((12, N)), pltpu.SemaphoreType.DMA((12, N)),
        ]
        vmem = pl.BlockSpec(memory_space=pltpu.VMEM)
        return pl.pallas_call(
            functools.partial(kernel, axis),
            out_shape=(jax.ShapeDtypeStruct((32, R, R), BF16), jax.ShapeDtypeStruct((8, R, W), BF16)),
            in_specs=[vmem] * len(args),
            out_specs=(vmem, vmem),
            scratch_shapes=scratch,
            compiler_params=pltpu.CompilerParams(collective_id=0, has_side_effects=True, vmem_limit_bytes=58 * 1024 * 1024),
        )(*args)

    in_specs = (P(('data', 'dap')), P(('data', 'dap')), P('data'), P('data')) + (P(),) * 13
    out_specs = (P(('data', 'dap')), P(('data', 'dap')))
    return jax.shard_map(local_step, mesh=mesh, in_specs=in_specs, out_specs=out_specs, check_vma=False)
```

profile of v0, /device:TPU:0, one launch (start us, length us, event | category | flops | bytes accessed | tf_op | source)
XLA Modules:
  0.0 141.4 jit_solution(9414464506539257658)
XLA Ops:
  0.6 138.2 %shard_map.176 = (bf16[32,64,64]{2,1,0:T(8,128)(2,1)}, bf16[8,64,128]{2,1,0:T(8,128)(2,1)}) custom-call(bf16[32,64,64]{2,1,0:T(8,128)(2,1)} %m_ref.1, bf16[8,64,128]{2,1,0:T(8,128)(2,1)} %z_ref.1, s32[64,256]{1,0:T(8,128)} %bitcast.30, s32[1,64]{1,0:T(1,128)} %bitcast.39, bf16[2,8,128]{2,1,0:T(8,128)(2,1)} %bitcast.36, bf16[2,256,64]{2,1,0:T(8,128)(2,1)} %bitcast.28, ...), custom_call_target="tpu_custom_call" | custom-call | tf_op jit(solution)/shard_map/pallas_call | solution.py:400
  138.9 0.0 copy-start
  138.9 1.9 %copy.21 = bf16[32,64,64]{2,1,0:T(8,128)(2,1)} copy(bf16[32,64,64]{2,1,0:T(8,128)(2,1)} %get-tuple-element.4) | data formatting | bytes 524288
  140.8 0.0 copy-done
  140.8 0.7 copy.22
Async XLA Ops:
  138.9 1.9 %copy-start = (bf16[8,64,128]{2,1,0:T(8,128)(2,1)S(1)}, bf16[8,64,128]{2,1,0:T(8,128)(2,1)}, u32[]{:S(2)}) copy-start(bf16[8,64,128]{2,1,0:T(8,128)(2,1)} %get-tuple-element.5) | copy-start | bytes 393220
where the time goes:
time: 142 us; the launch traced here: 141 us
  Pallas kernels  138 us (97%)
  local copies, waits for them, and re-layouts  2.56 us (2%)
    pallas_call x1, Pallas kernels, local_step(): pl.pallas_call(functools.partial(kernel, axis), out_shape=(jax.ShapeDtype...  138 us

commit v1 on v0

--- a/solution.py
+++ b/solution.py
@@ -11,8 +11,9 @@
 BF16 = jnp.bfloat16
 LOG2E = 1.4426950408889634
 NEG = -1e9
+NEG_PARTS = (-2835349504.0, 6914048.0, 8320.0)
 N = 8
-R, W, S = 64, 128, 256
+R, W, S, T, Q = 64, 128, 256, 512, 32
 
 PH_RB1, PH_M1, PH_C1, PH_SB1, PH_Z1, PH_EB1, PH_RB2, PH_C2, PH_M2, PH_EB2, PH_Z2, PH_SB2 = range(12)
 
@@ -49,30 +50,39 @@
     return (e * (1.0 / jnp.sum(e, axis=-2, keepdims=True))).astype(BF16)
 
 
-def attend_pair(proj, heads, dim, bias_ref, key_mask, hm_ref, rm_ref):
-    hd = heads * dim
-    q, k, v, g = (proj[n * hd:(n + 1) * hd] for n in range(4))
-    lo = low_lanes(hd)
+def pair_logits(q, k, heads, hm_ref):
+    lo = low_lanes(q.shape[0])
     qbd = jnp.concatenate([jnp.where(lo, q, 0.0), jnp.where(lo, 0.0, q)], axis=0).astype(BF16)
     kt = jnp.transpose(k)
     kp = jnp.concatenate([kt[0:R], kt[R:W]], axis=1).astype(BF16)
-    lhs = jnp.concatenate([kp] * heads, axis=0) * hm_ref[...]
-    s = mm(lhs, qbd)
-    x = s * (dim ** -0.5 * LOG2E) + bias_ref[...]
-    x = jnp.where(key_mask[None] > 0, x.reshape(heads, R, W), NEG * LOG2E)
-    p = softmax_keys(x).reshape(heads * R, W)
+    return mm(jnp.concatenate([kp] * heads, axis=0) * hm_ref[...], qbd)
+
+
+def pair_probs(s_ref, p_ref, heads, dim, bias_ref, key_mask):
+    masked = key_mask > 0
+    for h in range(heads):
+        rows = slice(R * h, R * h + R)
+        x = s_ref[rows, :] * (dim ** -0.5 * LOG2E) + bias_ref[rows, :]
+        p_ref[rows, :] = softmax_keys(jnp.where(masked, x, NEG * LOG2E))
+
+
+def pair_values(v, p_ref, heads, rm_ref):
+    hd = v.shape[0]
+    lo = low_lanes(hd)
     vr = pltpu.roll(v, R, 1)
     v2 = jnp.concatenate([jnp.where(lo, v, vr), jnp.where(lo, vr, v)], axis=0).astype(BF16)
-    vm = jnp.concatenate([v2] * (heads // 2), axis=1) * rm_ref[...]
-    o2 = mm(vm, p)
-    o = jnp.where(lo, o2[0:hd], o2[hd:2 * hd])
+    o2 = mm(jnp.concatenate([v2] * (heads // 2), axis=1) * rm_ref[...], p_ref[...])
+    return jnp.where(lo, o2[0:hd], o2[hd:2 * hd])
+
+
+def gate(o, g):
     return (o * jax.nn.sigmoid(g)).astype(BF16)
 
 
 def kernel(axis, m_ref, z_ref, mt_ref, r_ref, wrb, wri, wro, wci, wco, woi, woo, wsb, wsi, wso, web, wei, weo, mo_ref, zo_ref,
-           maskb, mp, mloc, rn, rkey, hm_r, rm_r, hm_t, rm_t, wro_t, wco_t, wso_t, weo_t, wall, wf,
+           mp, mloc, rn, rkey, hm_r, rm_r, hm_t, rm_t, wro_t, wco_t, wso_t, weo_t, wall, wf,
            rowf, sm1, rm1, m1, sm2, rm2, aloc, remf, rem, cg, xop, zst, zf, sz, rz, pb,
-           bm_r1, bm_r2, br_r1, br_r2, bm_s1, bm_s2, bm_e1, bm_e2, br_s1, br_s2, br_e1, br_e2, bt_r, bt_t, pq, send, recv):
+           bm_r1, bm_r2, br_r1, br_r2, bm_s1, bm_s2, bm_e1, bm_e2, br_s1, br_s2, br_e1, br_e2, bt_r, bt_t, pq, sbuf, pbuf, pqm, xres, obuf, kaug, send, recv):
     me = lax.axis_index(axis)
     peers = [lax.rem(me + k, N) for k in range(N)]
     senders = [lax.rem(me + N - k, N) for k in range(N)]
@@ -135,23 +145,21 @@
         return jnp.concatenate(
             [jnp.transpose(zst[W * t:W * t + W, :].astype(F32)) for t in range(4)], axis=1)
 
-    zst[...] = z_ref[...].reshape(512, W)
+    zst[...] = z_ref[...].reshape(T, W)
     bias_message(ln(z_features()), wrb[0], 8, bm_r1)
     pl.semaphore_wait(barrier, N - 1)
     exchange(PH_RB1, lambda p: bm_r1, br_r1)
 
     mt = mt_ref[...].astype(F32)
     mt_b = mt.astype(BF16)
-    sel = (iota((S, W), 0) == 32 * me + iota((S, W), 1)) & (iota((S, W), 1) < 32)
+    sel = (iota((S, W), 0) == Q * me + iota((S, W), 1)) & (iota((S, W), 1) < Q)
     mloc[...] = mm(mt_b, jnp.where(sel, 1.0, 0.0).astype(BF16)).astype(BF16)
     mrows = mt_ref[pl.ds(pl.multiple_of(8 * me, 8), 8), :].astype(F32)
     t = iota((S, S), 1)
-    perm = iota((S, S), 0) == (t % W) // 16 * 32 + t // W * 16 + t % 16
+    perm = iota((S, S), 0) == (t % W) // 16 * Q + t // W * 16 + t % 16
     mperm = mm(mrows.astype(BF16), jnp.where(perm, 1.0, 0.0).astype(BF16))
     mp[...] = mperm
-    mpt = jnp.transpose(mperm)
     for i in range(8):
-        maskb[i] = jnp.broadcast_to(mpt[:, i:i + 1], (S, W))
         row = jnp.broadcast_to(mrows[i:i + 1, :], (W, S)).astype(BF16)
         rn[i] = 1.0 / (1e-3 + mm_nt(mt_b, row))
     rkey[...] = jnp.transpose(jnp.broadcast_to(r_ref[...].astype(F32), (W, R)))
@@ -161,65 +169,148 @@
 
     fill(hm_r, lambda r, c: r // R == (c % R) // 8)
     fill(rm_r, lambda r, c: (r % R) // 8 == c // R)
-    fill(hm_t, lambda r, c: r // R == (c % W) // 32)
-    fill(rm_t, lambda r, c: (r % W) // 32 == c // R)
+    fill(hm_t, lambda r, c: r // R == (c % W) // Q)
+    fill(rm_t, lambda r, c: (r % W) // Q == c // R)
     for b in range(2):
         wro_t[b] = jnp.transpose(wro[b].astype(F32)).astype(BF16)
         wco_t[b] = jnp.transpose(wco[b].astype(F32)).astype(BF16)
         wso_t[b] = jnp.transpose(wso[b].astype(F32)).astype(BF16)
         weo_t[b] = jnp.transpose(weo[b].astype(F32)).astype(BF16)
     wf[...] = woo[0].astype(F32)
-    for n in range(32):
+    for n in range(Q):
         a, b = n // 4, n % 4
-        wall[0, 32 * a:32 * a + 32, W * b:W * b + W] = wf[pl.ds(n, 32, stride=32), :].astype(BF16)
-        wall[1, 32 * a:32 * a + 32, W * b:W * b + W] = woo[1, 32 * n:32 * n + 32, :]
-
-    def row_attention(b, xt, pair):
-        proj = rnd(mm(wri[b], ln(xt)))
+        wall[0, Q * a:Q * a + Q, W * b:W * b + W] = wf[pl.ds(n, Q, stride=Q), :].astype(BF16)
+        wall[1, Q * a:Q * a + Q, W * b:W * b + W] = woo[1, Q * n:Q * n + Q, :]
+
+    def row_attention(b, load, store):
+        for c in range(4):
+            x = jnp.concatenate([load(4 * c + t) for t in range(4)], axis=1)
+            proj = rnd(mm(wri[b], ln(x)))
+            for t in range(4):
+                xres[4 * c + t] = x[:, W * t:W * t + W]
+                pqm[4 * c + t] = proj[:, W * t:W * t + W]
         r, c = iota((W, W), 0), iota((W, W), 1)
-        pick = r == jnp.where(c < R, pair, pair + 16)
-        key_mask = mm(mloc[...], jnp.where(pick, 1.0, 0.0).astype(BF16))
-        gated = attend_pair(proj, 8, 8, bt_r, key_mask, hm_r, rm_r)
-        return rnd(xt + mm(wro_t[b], gated))
+        cs = jnp.where(c < R, 0, 16)
+
+        def logits(pair, slot):
+            sbuf[slot] = pair_logits(pqm[pair, 0:R, :], pqm[pair, R:2 * R, :], 8, hm_r)
+
+        def probs(pair, slot):
+            key_mask = mm(mloc[...], jnp.where(r == cs + pair, 1.0, 0.0).astype(BF16))
+            pair_probs(sbuf.at[slot], pbuf.at[slot], 8, 8, bt_r, key_mask)
+
+        def values(pair, slot):
+            obuf[pair] = pair_values(pqm[pair, 2 * R:3 * R, :], pbuf.at[slot], 8, rm_r)
+
+        return logits, probs, values
+
+    def row_finish(b, store):
+        for c in range(4):
+            g = jnp.concatenate([pqm[4 * c + t, 3 * R:4 * R, :] for t in range(4)], axis=1)
+            o = jnp.concatenate([obuf[4 * c + t] for t in range(4)], axis=1)
+            x = jnp.concatenate([xres[4 * c + t] for t in range(4)], axis=1)
+            y = rnd(x + mm(wro_t[b], gate(o, g)))
+            for t in range(4):
+                store(4 * c + t, jnp.transpose(y[:, W * t:W * t + W]))
+
+    def row_stack(b, load, store):
+        logits, probs, values = row_attention(b, load, store)
+        logits(0, 0)
+
+        def step(n, carry):
+            logits(2 * n + 1, 1)
+            probs(2 * n, 0)
+            values(jnp.maximum(2 * n - 1, 0), 1)
+            logits(jnp.minimum(2 * n + 2, 15), 0)
+            probs(2 * n + 1, 1)
+            values(2 * n, 0)
+            return carry
+
+        pbuf[1] = jnp.zeros((T, W), BF16)
+        lax.fori_loop(0, 8, step, 0)
+        values(15, 1)
+        row_finish(b, store)
 
     arrive(PH_RB1, bm_r1, br_r1)
     bias_table(br_r1, 8, bt_r, False)
 
-    def row1(pair, carry):
-        x = jnp.concatenate([m_ref[pair], m_ref[pair + 16]], axis=0).astype(F32)
-        y = row_attention(0, jnp.transpose(x), pair)
-        yt = jnp.transpose(y)
-        rowf[pl.ds(pl.multiple_of(R * pair, R), R), :] = jnp.concatenate([yt[0:R], yt[R:W]], axis=1)
-        return carry
-
-    lax.fori_loop(0, 16, row1, 0)
+    def store1(pair, yt):
+        rowf[R * pair:R * pair + R, :] = jnp.concatenate([yt[0:R], yt[R:W]], axis=1)
+
+    row_stack(0, lambda pair: jnp.transpose(jnp.concatenate([m_ref[pair], m_ref[pair + 16]], axis=0).astype(F32)), store1)
     for i in range(R):
         sm1[i // 8, i % 8] = rowf[pl.ds(i, 16, stride=R), :].astype(BF16)
     exchange(PH_M1, lambda p: sm1.at[p], rm1)
 
-    def column_attention(b, xt, i):
-        proj = rnd(mm(wci[b], ln(xt)))
-        q, k, v, g = (proj[R * n:R * n + R] for n in range(4))
-        kt = jnp.transpose(k).astype(BF16)
+    def both(ref, i, rows=slice(None)):
+        return jnp.concatenate([ref[2 * i, rows, :], ref[2 * i + 1, rows, :]], axis=1)
+
+    def put(ref, i, value):
+        ref[2 * i] = value[:, 0:W]
+        ref[2 * i + 1] = value[:, W:S]
+
+    def column_project(b, load):
+        part = iota((R, S), 0)
+        flags = jnp.where(part == 0, NEG_PARTS[0], jnp.where(part == 1, NEG_PARTS[1], jnp.where(part == 2, NEG_PARTS[2], 0.0)))
+        for i in range(8):
+            x = load(i)
+            proj = rnd(mm(wci[b], ln(x)))
+            put(xres, i, x)
+            put(pqm, i, proj)
+            keep = mp[i:i + 1, :]
+            ka = jnp.concatenate([proj[R:2 * R] * keep, flags * (1.0 - keep)], axis=0)
+            kaug[i] = jnp.transpose(ka).astype(BF16)
+
+    def column_stack(b, load, finish):
+        column_project(b, load)
         head = iota((R, S), 0) // 8
-        key_mask = maskb[i] > 0
-        out = []
-        for h in range(8):
-            s = mm(kt, jnp.where(head == h, q, 0.0).astype(BF16))
-            vh = v[8 * h:8 * h + 8].astype(BF16)
-            parts = []
+        ones = jnp.where(iota((R, S), 0) < 3, 1.0, 0.0)
+
+        def logits(i, h, slot):
+            q = jnp.where(head == h, both(pqm, i, slice(0, R)), 0.0)
+            s = mm(kaug[i], jnp.concatenate([q, ones], axis=0).astype(BF16))
+            sbuf[slot, 0:S, :] = s[:, 0:W]
+            sbuf[slot, S:2 * S, :] = s[:, W:S]
+
+        def probs(slot):
             for n in range(2):
-                x = jnp.where(key_mask, s[:, W * n:W * n + W] * (8 ** -0.5 * LOG2E), NEG * LOG2E)
-                parts.append(softmax_keys(x))
-            out.append(mm(vh, jnp.concatenate(parts, axis=1)))
-        o = jnp.concatenate(out, axis=0)
-        gated = (o * jax.nn.sigmoid(g)).astype(BF16)
-        return rnd(xt + mm(wco_t[b], gated))
+                rows = slice(S * n, S * n + S)
+                pbuf[slot, rows, :] = softmax_keys(sbuf[slot, rows, :] * (8 ** -0.5 * LOG2E))
+
+        def values(i, h, slot):
+            rows = slice(2 * R + 8 * h, 2 * R + 8 * h + 8)
+            vh = both(pqm, i, rows).astype(BF16)
+            p = jnp.concatenate([pbuf[slot, 0:S, :], pbuf[slot, S:2 * S, :]], axis=1)
+            o = mm(vh, p)
+            obuf[2 * i, 8 * h:8 * h + 8, :] = o[:, 0:W]
+            obuf[2 * i + 1, 8 * h:8 * h + 8, :] = o[:, W:S]
+
+        pbuf[1] = jnp.zeros((T, W), BF16)
+        logits(0, 0, 0)
+
+        def step(i, carry):
+            for h in range(8):
+                if h < 7:
+                    logits(i, h + 1, (h + 1) % 2)
+                else:
+                    logits(jnp.minimum(i + 1, 7), 0, 0)
+                probs(h % 2)
+                if h == 0:
+                    values(jnp.maximum(i - 1, 0), 7, 1)
+                else:
+                    values(i, h - 1, (h - 1) % 2)
+            return carry
+
+        lax.fori_loop(0, 8, step, 0)
+        values(7, 7, 1)
+        for i in range(8):
+            y = rnd(both(xres, i) + mm(wco_t[b], gate(both(obuf, i), both(pqm, i, slice(3 * R, 4 * R)))))
+            finish(i, y)
 
     def opm_operands(b, xt, i):
-        proj = mm(woi[b], ln(xt)) * mp[pl.ds(i, 1), :]
-        near, far = (proj[0:32], proj[32:R]) if b == 0 else (proj[32:R], proj[0:32])
-        rows = pl.ds(pl.multiple_of(32 * i, 32), 32)
+        proj = mm(woi[b], ln(xt)) * mp[i:i + 1, :]
+        near, far = (proj[0:Q], proj[Q:R]) if b == 0 else (proj[Q:R], proj[0:Q])
+        rows = slice(Q * i, Q * i + Q)
         aloc[b, rows, :] = near.astype(BF16)
         remf[0, rows, :] = far[:, 0:W]
         remf[1, rows, :] = far[:, W:S]
@@ -228,42 +319,40 @@
         for n in range(16):
             for t in range(2):
                 rem[b, 16 * n:16 * n + 16, W * t:W * t + W] = jnp.concatenate(
-                    [remf[t, pl.ds(2 * n + u, 8, stride=32), :] for u in range(2)], axis=0).astype(BF16)
+                    [remf[t, pl.ds(2 * n + u, 8, stride=Q), :] for u in range(2)], axis=0).astype(BF16)
 
     arrive(PH_M1, sm1.at[0], rm1)
 
-    def col1(i, carry):
-        x = rm1[:, i].reshape(W, W).astype(F32)
-        xt = jnp.transpose(x)
-        y = column_attention(0, jnp.concatenate([xt[0:R], xt[R:W]], axis=1), i)
+    def load1(i):
+        xt = jnp.transpose(rm1[:, i].reshape(W, W).astype(F32))
+        return jnp.concatenate([xt[0:R], xt[R:W]], axis=1)
+
+    def finish1(i, y):
         m1[i] = y.astype(BF16)
         opm_operands(0, y, i)
-        return carry
-
-    lax.fori_loop(0, 8, col1, 0)
+
+    column_stack(0, load1, finish1)
     pack_far(0)
     exchange(PH_C1, lambda p: rem.at[0], cg.at[0])
 
-    def col2(i, carry):
-        y = column_attention(1, m1[i].astype(F32), i)
+    def finish2(i, y):
         opm_operands(1, y, i)
         yt = jnp.transpose(jnp.concatenate([y[:, 0:W], y[:, W:S]], axis=0)).astype(BF16)
         sm2[:, i] = yt.reshape(8, 16, W)
-        return carry
-
-    lax.fori_loop(0, 8, col2, 0)
+
+    column_stack(1, lambda i: m1[i].astype(F32), finish2)
     exchange(PH_M2, lambda p: sm2.at[p], rm2)
     pack_far(1)
 
     def opm(b):
         for n in range(8):
-            far = cg[b, :, 32 * n:32 * n + 32, :].reshape(S, S)
+            far = cg[b, :, Q * n:Q * n + Q, :].reshape(S, S)
             o = mm_nt(aloc[b], far).astype(BF16)
             for i in range(8):
-                xop[i, 32 * n:32 * n + 32, :] = o[32 * i:32 * i + 32, :]
+                xop[i, Q * n:Q * n + Q, :] = o[Q * i:Q * i + Q, :]
 
         def one(i, carry):
-            y = mm(jnp.transpose(xop[i]), wall[b]).reshape(8, 4, 8, 512)
+            y = mm(jnp.transpose(xop[i]), wall[b]).reshape(8, 4, 8, T)
             u = sum(y[:, n, :, W * n:W * n + W] for n in range(4)).reshape(R, W)
             rows = pl.ds(pl.multiple_of(R * i, R), R)
             zst[rows, :] = (zst[rows, :].astype(F32) + u * rn[i]).astype(BF16)
@@ -275,16 +364,20 @@
         pq[...] = rnd(mm(w_in, xln))
 
     def tri_attend(x, w_out_t):
-        out = []
+        def part(n, t):
+            return pq[W * n:W * n + W, W * t:W * t + W]
+
         for t in range(4):
-            gated = attend_pair(pq[:, W * t:W * t + W], 4, 32, bt_t, rkey[...], hm_t, rm_t)
-            out.append(rnd(x[:, W * t:W * t + W] + mm(w_out_t, gated)))
-        return jnp.concatenate(out, axis=1)
+            sbuf[t, 0:S, :] = pair_logits(part(0, t), part(1, t), 4, hm_t)
+        for t in range(4):
+            pair_probs(sbuf.at[t], pbuf.at[t], 4, Q, bt_t, rkey[...])
+        o = jnp.concatenate([pair_values(part(2, t), pbuf.at[t, 0:S], 4, rm_t) for t in range(4)], axis=1)
+        return rnd(x + mm(w_out_t, gate(o, pq[3 * W:4 * W, :])))
 
     def swap_pair(y, n):
         for t in range(4):
             zf[W * t:W * t + W, :] = jnp.transpose(y[:, W * t:W * t + W])
-        for c in range(32):
+        for c in range(Q):
             sz[n, 16 * c:16 * c + 16, :] = jnp.concatenate(
                 [zf[pl.ds(2 * c, 8, stride=R), :], zf[pl.ds(2 * c + 1, 8, stride=R), :]], axis=0).astype(BF16)
 
@@ -336,15 +429,15 @@
     bias_table(br_r2, 8, bt_r, True)
     rowf[...] = rm2[...].reshape(1024, W).astype(F32)
 
-    def row2(pair, carry):
+    def load2(pair):
         xt = jnp.transpose(rowf[pl.ds(pair, R, stride=16), :])
-        xm = jnp.concatenate([xt[0:R], xt[R:W]], axis=1)
-        yt = jnp.transpose(row_attention(1, xm, pair)).astype(BF16)
-        mo_ref[pair] = yt[0:R]
-        mo_ref[pair + 16] = yt[R:W]
-        return carry
-
-    lax.fori_loop(0, 16, row2, 0)
+        return jnp.concatenate([xt[0:R], xt[R:W]], axis=1)
+
+    def store2(pair, yt):
+        mo_ref[pair] = yt[0:R].astype(BF16)
+        mo_ref[pair + 16] = yt[R:W].astype(BF16)
+
+    row_stack(1, load2, store2)
 
     arrive(PH_EB2, bm_e2, br_e2)
     bias_table(br_e2, 4, bt_t, False)
@@ -382,24 +475,25 @@
                 tin(w_te_bias), tin(w_te_in), w_te_out.reshape(2, W, W))
         v = pltpu.VMEM
         scratch = [
-            v((8, S, W), F32), v((8, S), F32), v((R, W), BF16), v((8, R, W), F32), v((R, W), F32),
-            v((512, W), BF16), v((W, 512), BF16), v((S, S), BF16), v((S, S), BF16),
+            v((8, S), F32), v((R, W), BF16), v((8, R, W), F32), v((R, W), F32),
+            v((T, W), BF16), v((W, T), BF16), v((S, S), BF16), v((S, S), BF16),
             v((2, R, R), BF16), v((2, R, R), BF16), v((2, W, W), BF16), v((2, W, W), BF16),
-            v((2, S, 512), BF16), v((1024, W), F32),
+            v((2, S, T), BF16), v((1024, W), F32),
             v((1024, W), F32), v((8, 8, 16, W), BF16), v((8, 8, 16, W), BF16), v((8, R, S), BF16),
             v((8, 8, 16, W), BF16), v((8, 8, 16, W), BF16),
             v((2, S, S), BF16), v((2, S, W), F32), v((2, S, S), BF16), v((2, 8, S, S), BF16), v((8, S, S), BF16),
-            v((512, W), BF16), v((512, W), F32), v((2, 512, W), BF16), v((2, 8, R, W), BF16), v((R, W), F32),
-            v((32, W), BF16), v((32, W), BF16), v((8, 32, W), BF16), v((8, 32, W), BF16),
+            v((T, W), BF16), v((T, W), F32), v((2, T, W), BF16), v((2, 8, R, W), BF16), v((R, W), F32),
+            v((Q, W), BF16), v((Q, W), BF16), v((8, Q, W), BF16), v((8, Q, W), BF16),
             v((16, W), BF16), v((16, W), BF16), v((16, W), BF16), v((16, W), BF16),
             v((8, 16, W), BF16), v((8, 16, W), BF16), v((8, 16, W), BF16), v((8, 16, W), BF16),
-            v((512, W), F32), v((S, W), F32), v((512, 512), F32),
+            v((T, W), F32), v((S, W), F32), v((T, T), F32),
+            v((4, T, W), F32), v((4, T, W), BF16), v((16, S, W), F32), v((16, R, W), F32), v((16, R, W), F32), v((8, S, W), BF16),
             pltpu.SemaphoreType.DMA((12, N)), pltpu.SemaphoreType.DMA((12, N)),
         ]
         vmem = pl.BlockSpec(memory_space=pltpu.VMEM)
         return pl.pallas_call(
             functools.partial(kernel, axis),
-            out_shape=(jax.ShapeDtypeStruct((32, R, R), BF16), jax.ShapeDtypeStruct((8, R, W), BF16)),
+            out_shape=(jax.ShapeDtypeStruct((Q, R, R), BF16), jax.ShapeDtypeStruct((8, R, W), BF16)),
             in_specs=[vmem] * len(args),
             out_specs=(vmem, vmem),
             scratch_shapes=scratch,

time: 142 us -> 86.6 us (0.61)
  Pallas kernels: 138 us -> 83.2 us
    pallas_call x1, Pallas kernels: 138 us -> 83.2 us  [local_step(): pl.pallas_call(functools.partial(kernel, axis), out_shape=(jax.ShapeDtype...]
where the time goes in v1:
time: 86.6 us; the launch traced here: 86.4 us
  Pallas kernels  83.2 us (96%)
  local copies, waits for them, and re-layouts  2.56 us (3%)
    pallas_call x1, Pallas kernels, local_step(): pl.pallas_call(functools.partial(kernel, axis), out_shape=(jax.ShapeDtype...  83.2 us
    unnamed x4, local copies, waits for them, and re-layouts  2.56 us

profile of v1, /device:TPU:0, one launch (start us, length us, event | category | flops | bytes accessed | tf_op | source)
XLA Modules:
  0.0 86.4 jit_solution(2659205217560154735)
XLA Ops:
  0.6 83.2 %shard_map.176 = (bf16[32,64,64]{2,1,0:T(8,128)(2,1)}, bf16[8,64,128]{2,1,0:T(8,128)(2,1)}) custom-call(bf16[32,64,64]{2,1,0:T(8,128)(2,1)} %m_ref.1, bf16[8,64,128]{2,1,0:T(8,128)(2,1)} %z_ref.1, s32[64,256]{1,0:T(8,128)} %bitcast.30, s32[1,64]{1,0:T(1,128)} %bitcast.39, bf16[2,8,128]{2,1,0:T(8,128)(2,1)} %bitcast.36, bf16[2,256,64]{2,1,0:T(8,128)(2,1)} %bitcast.28, ...), custom_call_target="tpu_custom_call" | custom-call | tf_op jit(solution)/shard_map/pallas_call | solution.py:494
  83.9 0.0 copy-start
  83.9 1.9 %copy.21 = bf16[32,64,64]{2,1,0:T(8,128)(2,1)} copy(bf16[32,64,64]{2,1,0:T(8,128)(2,1)} %get-tuple-element.4) | data formatting | bytes 524288
  85.8 0.0 copy-done
  85.8 0.7 copy.22
Async XLA Ops:
  83.9 1.9 %copy-start = (bf16[8,64,128]{2,1,0:T(8,128)(2,1)S(1)}, bf16[8,64,128]{2,1,0:T(8,128)(2,1)}, u32[]{:S(2)}) copy-start(bf16[8,64,128]{2,1,0:T(8,128)(2,1)} %get-tuple-element.5) | copy-start | bytes 393220

commit v2 on v1

v2 whole, which is shorter than its diff:
```python
import functools

import jax
import jax.numpy as jnp
from jax import lax
from jax.experimental import pallas as pl
from jax.experimental.pallas import tpu as pltpu
from jax.sharding import PartitionSpec as P

F32 = jnp.float32
BF16 = jnp.bfloat16
LOG2E = 1.4426950408889634
NEG = -1e9
NEG_PARTS = (-2835349504.0, 6914048.0, 8320.0)
N = 8
R, W, S, T, Q = 64, 128, 256, 512, 32

PH_RB1, PH_M1, PH_C1, PH_SB1, PH_Z1, PH_EB1, PH_RB2, PH_C2, PH_M2, PH_EB2, PH_Z2, PH_SB2 = range(12)


def mm(a, b):
    return jnp.dot(a, b, preferred_element_type=F32)


def mm_nt(a, b):
    return lax.dot_general(a, b, (((1,), (1,)), ((), ())), preferred_element_type=F32)


def iota(shape, dim):
    return lax.broadcasted_iota(jnp.int32, shape, dim)


def ln(x):
    mu = jnp.mean(x, axis=0, keepdims=True)
    c = x - mu
    var = jnp.mean(c * c, axis=0, keepdims=True)
    return (c * lax.rsqrt(var + 1e-5)).astype(BF16)


def rnd(x):
    return x.astype(BF16).astype(F32)


def low_lanes(rows):
    return iota((rows, W), 1) < R


def softmax_keys(x, scale):
    e = jnp.exp2((x - jnp.max(x, axis=-2, keepdims=True)) * scale)
    return (e * (1.0 / jnp.sum(e, axis=-2, keepdims=True))).astype(BF16)


def pair_logits(q, k, heads, hm_ref):
    lo = low_lanes(q.shape[0])
    qbd = jnp.concatenate([jnp.where(lo, q, 0.0), jnp.where(lo, 0.0, q)], axis=0).astype(BF16)
    kt = jnp.transpose(k)
    kp = jnp.concatenate([kt[0:R], kt[R:W]], axis=1).astype(BF16)
    return mm(jnp.concatenate([kp] * heads, axis=0) * hm_ref[...], qbd)


def pair_probs(s_ref, p_ref, heads, dim, bias_ref, key_mask):
    masked = key_mask > 0
    for h in range(heads):
        rows = slice(R * h, R * h + R)
        x = s_ref[rows, :] * dim ** -0.5 + bias_ref[rows, :]
        p_ref[rows, :] = softmax_keys(jnp.where(masked, x, NEG), LOG2E)


def pair_values(v, p_ref, heads, rm_ref):
    hd = v.shape[0]
    lo = low_lanes(hd)
    vr = pltpu.roll(v, R, 1)
    v2 = jnp.concatenate([jnp.where(lo, v, vr), jnp.where(lo, vr, v)], axis=0).astype(BF16)
    o2 = mm(jnp.concatenate([v2] * (heads // 2), axis=1) * rm_ref[...], p_ref[...])
    return jnp.where(lo, o2[0:hd], o2[hd:2 * hd])


def gate(o, g):
    return (o * jax.nn.sigmoid(g)).astype(BF16)


def kernel(axis, m_ref, z_ref, mt_ref, r_ref, wrb, wri, wro, wci, wco, woi, woo, wsb, wsi, wso, web, wei, weo, mo_ref, zo_ref,
           mp, mloc, rn, rkey, hm_r, rm_r, hm_t, rm_t, wro_t, wco_t, wso_t, weo_t, wall, wf,
           rowf, sm1, rm1, m1, sm2, rm2, aloc, remf, rem, cg, xop, zst, zf, sz, rz, pb,
           bm_r1, bm_r2, br_r1, br_r2, bm_s1, bm_s2, bm_e1, bm_e2, br_s1, br_s2, br_e1, br_e2, bt_r, bt_t, pq, sbuf, pbuf, pqm, xres, obuf, kaug, stri, ptri, send, recv):
    me = lax.axis_index(axis)
    peers = [lax.rem(me + k, N) for k in range(N)]
    senders = [lax.rem(me + N - k, N) for k in range(N)]

    def copy(ph, k, src, dst):
        return pltpu.make_async_remote_copy(
            src_ref=src, dst_ref=dst, send_sem=send.at[ph, k], recv_sem=recv.at[ph, k],
            device_id={axis: peers[k]}, device_id_type=pl.DeviceIdType.MESH)

    started = []

    chip, core = me // 2, lax.rem(me, 2)
    mate = me + 1 - 2 * core
    chip_x = chip + 1 - 2 * lax.rem(chip, 2)
    chips = [chip_x, lax.rem(chip + 2, 4), lax.rem(chip_x + 2, 4)]

    def send_to(ph, n, src, dst, device):
        return pltpu.make_async_remote_copy(
            src_ref=src, dst_ref=dst, send_sem=send.at[ph, n], recv_sem=recv.at[ph, n],
            device_id={axis: device}, device_id_type=pl.DeviceIdType.MESH)

    def far_copy(ph, b, n):
        to, slot = (2 * chips[n] + core, me) if n < 3 else (mate, me) if n == 3 else (mate, 2 * chips[n - 4] + core)
        return send_to(ph, n, rem.at[b] if n <= 3 else cg.at[b, slot], cg.at[b, slot], to)

    def far_start(ph, b, ns):
        for n in ns:
            far_copy(ph, b, n).start()
            started.append(functools.partial(far_copy, ph, b, n))

    def far_forward(ph, b):
        for n in range(3):
            send_to(ph, n, rem.at[b], cg.at[b, 2 * chips[n] + core], mate).wait_recv()
        far_start(ph, b, (4, 5, 6))

    def far_arrive(ph, b):
        send_to(ph, 3, rem.at[b], cg.at[b, mate], mate).wait_recv()
        for n in range(3):
            send_to(ph, 4 + n, rem.at[b], cg.at[b, 2 * chips[n] + 1 - core], mate).wait_recv()

    def exchange(ph, src_of, dst_ref):
        for k in range(1, N):
            c = functools.partial(copy, ph, k, src_of(peers[k]), dst_ref.at[me])
            c().start()
            started.append(c)
        dst_ref[me] = src_of(me)[...]

    def arrive(ph, like, dst_ref):
        for k in range(1, N):
            copy(ph, k, like, dst_ref.at[senders[k]]).wait_recv()

    barrier = pltpu.get_barrier_semaphore()
    for k in range(1, N):
        pl.semaphore_signal(barrier, inc=1, device_id={axis: peers[k]}, device_id_type=pl.DeviceIdType.MESH)

    def bias_message(xln, w_bias, heads, msg):
        half = heads // 2
        b = mm(w_bias, xln)
        if heads == 4:
            b = jnp.concatenate([b, b], axis=0)
        bh = pltpu.roll(b, N - half, 0)
        lo = low_lanes(N)
        for i in range(N):
            bl_v = b[:, W * (i // 2):W * (i // 2) + W]
            bh_v = bh[:, W * (i // 2):W * (i // 2) + W]
            if i % 2 == 0:
                pb[N * i:N * i + N, :] = jnp.where(lo, bl_v, pltpu.roll(bh_v, R, 1))
            else:
                pb[N * i:N * i + N, :] = jnp.where(lo, pltpu.roll(bl_v, R, 1), bh_v)
        msg[...] = jnp.concatenate([pb[pl.ds(h, N, stride=N), :] for h in range(half)], axis=0).astype(BF16)

    def bias_table(got, heads, table, gathered_keys):
        half = heads // 2
        full = got[...].astype(F32)
        for h in range(half):
            x = full[:, N * h:N * h + N, :].reshape(R, W)
            if gathered_keys:
                xr = pltpu.roll(x, R, 1)
                lo = low_lanes(R)
                table[R * h:R * h + R, :] = jnp.where(lo, x, xr)
                table[R * (half + h):R * (half + h) + R, :] = jnp.where(lo, xr, x)
            else:
                t = jnp.transpose(x)
                for hp in range(2):
                    blk = t[R * hp:R * hp + R]
                    table[R * (half * hp + h):R * (half * hp + h) + R, :] = jnp.concatenate([blk, blk], axis=1)

    def z_features():
        return jnp.concatenate(
            [jnp.transpose(zst[W * t:W * t + W, :].astype(F32)) for t in range(4)], axis=1)

    zst[...] = z_ref[...].reshape(T, W)
    bias_message(ln(z_features()), wrb[0], N, bm_r1)
    pl.semaphore_wait(barrier, N - 1)
    exchange(PH_RB1, lambda p: bm_r1, br_r1)

    def fill(ref, fn):
        ref[...] = jnp.where(fn(iota(ref.shape, 0), iota(ref.shape, 1)), 1.0, 0.0).astype(BF16)

    def row_constants():
        mt_b = mt_ref[...].astype(F32).astype(BF16)
        sel = (iota((S, W), 0) == Q * me + iota((S, W), 1)) & (iota((S, W), 1) < Q)
        mloc[...] = mm(mt_b, jnp.where(sel, 1.0, 0.0).astype(BF16)).astype(BF16)
        fill(hm_r, lambda r, c: r // R == (c % R) // N)
        fill(rm_r, lambda r, c: (r % R) // N == c // R)
        for b in range(2):
            wro_t[b] = jnp.transpose(wro[b].astype(F32)).astype(BF16)

    def other_constants():
        mt_b = mt_ref[...].astype(F32).astype(BF16)
        mrows = mt_ref[pl.ds(pl.multiple_of(N * me, N), N), :].astype(F32)
        t = iota((S, S), 1)
        perm = iota((S, S), 0) == (t % W) // 16 * Q + t // W * 16 + t % 16
        mp[...] = mm(mrows.astype(BF16), jnp.where(perm, 1.0, 0.0).astype(BF16))
        for i in range(N):
            row = jnp.broadcast_to(mrows[i:i + 1, :], (W, S)).astype(BF16)
            rn[i] = 1.0 / (1e-3 + mm_nt(mt_b, row))
        rkey[...] = jnp.transpose(jnp.broadcast_to(r_ref[...].astype(F32), (W, R)))
        fill(hm_t, lambda r, c: r // R == (c % W) // Q)
        fill(rm_t, lambda r, c: (r % W) // Q == c // R)
        for b in range(2):
            wco_t[b] = jnp.transpose(wco[b].astype(F32)).astype(BF16)
            wso_t[b] = jnp.transpose(wso[b].astype(F32)).astype(BF16)
            weo_t[b] = jnp.transpose(weo[b].astype(F32)).astype(BF16)
        wf[...] = woo[0].astype(F32)
        for n in range(Q):
            a, b = n // 4, n % 4
            wall[0, Q * a:Q * a + Q, W * b:W * b + W] = wf[pl.ds(n, Q, stride=Q), :].astype(BF16)
            wall[1, Q * a:Q * a + Q, W * b:W * b + W] = woo[1, Q * n:Q * n + Q, :]

    def row_project(b, load):
        for c in range(4):
            x = jnp.concatenate([load(4 * c + t) for t in range(4)], axis=1)
            proj = rnd(mm(wri[b], ln(x)))
            for t in range(4):
                xres[4 * c + t] = x[:, W * t:W * t + W]
                pqm[4 * c + t] = proj[:, W * t:W * t + W]

    def row_loop(lo, hi):
        r, c = iota((W, W), 0), iota((W, W), 1)
        cs = jnp.where(c < R, 0, 16)

        def logits(pair, slot):
            sbuf[slot] = pair_logits(pqm[pair, 0:R, :], pqm[pair, R:2 * R, :], N, hm_r)

        def probs(pair, slot):
            key_mask = mm(mloc[...], jnp.where(r == cs + pair, 1.0, 0.0).astype(BF16))
            pair_probs(sbuf.at[slot], pbuf.at[slot], N, N, bt_r, key_mask)

        def values(pair, slot):
            obuf[pair] = pair_values(pqm[pair, 2 * R:3 * R, :], pbuf.at[slot], N, rm_r)

        def step(n, carry):
            for t in range(4):
                p = 4 * n + t
                logits(jnp.minimum(p + 2, 15), (t + 2) % 4)
                probs(p, t)
                values(jnp.maximum(p - 1, 0), (t + 3) % 4)
            return carry

        if lo == 0:
            pbuf[3] = jnp.zeros((T, W), BF16)
            logits(0, 0)
            logits(1, 1)
        lax.fori_loop(lo, hi, step, 0)
        if hi == 4:
            values(15, 3)

    def row_finish(b, store):
        for c in range(4):
            g = jnp.concatenate([pqm[4 * c + t, 3 * R:4 * R, :] for t in range(4)], axis=1)
            o = jnp.concatenate([obuf[4 * c + t] for t in range(4)], axis=1)
            x = jnp.concatenate([xres[4 * c + t] for t in range(4)], axis=1)
            y = rnd(x + mm(wro_t[b], gate(o, g)))
            for t in range(4):
                store(4 * c + t, jnp.transpose(y[:, W * t:W * t + W]))

    row_constants()
    row_project(0, lambda pair: jnp.transpose(jnp.concatenate([m_ref[pair], m_ref[pair + 16]], axis=0).astype(F32)))
    arrive(PH_RB1, bm_r1, br_r1)
    bias_table(br_r1, N, bt_r, False)
    row_loop(0, 4)

    def store1(pair, yt):
        rowf[R * pair:R * pair + R, :] = jnp.concatenate([yt[0:R], yt[R:W]], axis=1)

    row_finish(0, store1)
    for i in range(R):
        sm1[i // N, i % N] = rowf[pl.ds(i, 16, stride=R), :].astype(BF16)
    exchange(PH_M1, lambda p: sm1.at[p], rm1)
    other_constants()

    def both(ref, i, rows=slice(None)):
        return jnp.concatenate([ref[2 * i, rows, :], ref[2 * i + 1, rows, :]], axis=1)

    def put(ref, i, value):
        ref[2 * i] = value[:, 0:W]
        ref[2 * i + 1] = value[:, W:S]

    def column_project(b, load):
        part = iota((R, S), 0)
        flags = jnp.where(part == 0, NEG_PARTS[0], jnp.where(part == 1, NEG_PARTS[1], jnp.where(part == 2, NEG_PARTS[2], 0.0)))
        for i in range(N):
            x = load(i)
            proj = rnd(mm(wci[b], ln(x)))
            put(xres, i, x)
            put(pqm, i, proj)
            keep = mp[i:i + 1, :]
            ka = jnp.concatenate([proj[R:2 * R] * keep, flags * (1.0 - keep)], axis=0)
            kaug[i] = jnp.transpose(ka).astype(BF16)

    def column_stack(b, load, finish, midway=None):
        column_project(b, load)
        head = iota((R, S), 0) // N
        ones = jnp.where(iota((R, S), 0) < 3, 1.0, 0.0)

        def logits(i, h, slot):
            q = jnp.where(head == h, both(pqm, i, slice(0, R)), 0.0)
            s = mm(kaug[i], jnp.concatenate([q, ones], axis=0).astype(BF16))
            sbuf[slot, 0:S, :] = s[:, 0:W]
            sbuf[slot, S:2 * S, :] = s[:, W:S]

        def probs(slot):
            for n in range(2):
                rows = slice(S * n, S * n + S)
                pbuf[slot, rows, :] = softmax_keys(sbuf[slot, rows, :], N ** -0.5 * LOG2E)

        def values(i, h, slot):
            rows = slice(2 * R + N * h, 2 * R + N * h + N)
            vh = both(pqm, i, rows).astype(BF16)
            p = jnp.concatenate([pbuf[slot, 0:S, :], pbuf[slot, S:2 * S, :]], axis=1)
            o = mm(vh, p)
            obuf[2 * i, N * h:N * h + N, :] = o[:, 0:W]
            obuf[2 * i + 1, N * h:N * h + N, :] = o[:, W:S]

        pbuf[3] = jnp.zeros((T, W), BF16)
        logits(0, 0, 0)
        logits(0, 1, 1)

        def step(i, carry):
            later = jnp.minimum(i + 1, 7)
            if midway is not None:
                pl.when(i == 6)(midway)
            for h in range(N):
                logits(i if h < 6 else later, (h + 2) % N, (h + 2) % 4)
                probs(h % 4)
                values(jnp.maximum(i - 1, 0) if h == 0 else i, (h + 7) % N, (h + 3) % 4)
            return carry

        lax.fori_loop(0, N, step, 0)
        values(7, 7, 3)
        for i in range(N):
            y = rnd(both(xres, i) + mm(wco_t[b], gate(both(obuf, i), both(pqm, i, slice(3 * R, 4 * R)))))
            finish(i, y)

    def opm_operands(b, xt, i):
        proj = mm(woi[b], ln(xt)) * mp[i:i + 1, :]
        near, far = (proj[0:Q], proj[Q:R]) if b == 0 else (proj[Q:R], proj[0:Q])
        rows = slice(Q * i, Q * i + Q)
        aloc[b, rows, :] = near.astype(BF16)
        remf[0, rows, :] = far[:, 0:W]
        remf[1, rows, :] = far[:, W:S]

    def pack_far(b):
        for n in range(16):
            for t in range(2):
                rem[b, 16 * n:16 * n + 16, W * t:W * t + W] = jnp.concatenate(
                    [remf[t, pl.ds(2 * n + u, N, stride=Q), :] for u in range(2)], axis=0).astype(BF16)

    arrive(PH_M1, sm1.at[0], rm1)

    def load1(i):
        xt = jnp.transpose(rm1[:, i].reshape(W, W).astype(F32))
        return jnp.concatenate([xt[0:R], xt[R:W]], axis=1)

    def finish1(i, y):
        m1[i] = y.astype(BF16)
        opm_operands(0, y, i)

    column_stack(0, load1, finish1)
    pack_far(0)
    far_start(PH_C1, 0, (0, 1, 2, 3))
    cg[0, me] = rem[0]

    def finish2(i, y):
        opm_operands(1, y, i)
        yt = jnp.transpose(jnp.concatenate([y[:, 0:W], y[:, W:S]], axis=0)).astype(BF16)
        sm2[:, i] = yt.reshape(N, 16, W)

    column_stack(1, lambda i: m1[i].astype(F32), finish2, lambda: far_forward(PH_C1, 0))
    pack_far(1)

    def opm(b):
        for n in range(N):
            far = cg[b, :, Q * n:Q * n + Q, :].reshape(S, S)
            o = mm_nt(aloc[b], far).astype(BF16)
            for i in range(N):
                xop[i, Q * n:Q * n + Q, :] = o[Q * i:Q * i + Q, :]

        for i in range(N):
            y = mm(jnp.transpose(xop[i]), wall[b]).reshape(N, 4, N, T)
            u = sum(y[:, n, :, W * n:W * n + W] for n in range(4)).reshape(R, W)
            rows = slice(R * i, R * i + R)
            zst[rows, :] = (zst[rows, :].astype(F32) + u * rn[i]).astype(BF16)

    def tri_project(xln, w_in):
        pq[...] = rnd(mm(w_in, xln))

    def tri_attend(x, w_out_t):
        def part(n, t):
            return pq[W * n:W * n + W, W * t:W * t + W]

        for t in range(4):
            stri[t] = pair_logits(part(0, t), part(1, t), 4, hm_t)
        for t in range(4):
            pair_probs(stri.at[t], ptri.at[t], 4, Q, bt_t, rkey[...])
        o = jnp.concatenate([pair_values(part(2, t), ptri.at[t], 4, rm_t) for t in range(4)], axis=1)
        return rnd(x + mm(w_out_t, gate(o, pq[3 * W:4 * W, :])))

    def swap_pair(y, n):
        for t in range(4):
            zf[W * t:W * t + W, :] = jnp.transpose(y[:, W * t:W * t + W])
        for c in range(Q):
            sz[n, 16 * c:16 * c + 16, :] = jnp.concatenate(
                [zf[pl.ds(2 * c, N, stride=R), :], zf[pl.ds(2 * c + 1, N, stride=R), :]], axis=0).astype(BF16)

    def take_pair(n):
        x = rz[n].astype(F32).reshape(N, N, N, W)
        for j in range(N):
            zst[R * j:R * j + R, :] = x[:, j].reshape(R, W).astype(BF16)

    def z_block(n, p):
        return sz.at[n, pl.ds(pl.multiple_of(R * p, R), R), :]

    far_arrive(PH_C1, 0)
    far_start(PH_C2, 1, (0, 1, 3))
    cg[1, me] = rem[1]
    opm(0)
    x = z_features()
    xln = ln(x)
    bias_message(xln, wsb[0], 4, bm_s1)
    exchange(PH_SB1, lambda p: bm_s1, br_s1)
    far_start(PH_C2, 1, (2,))
    tri_project(xln, wsi[0])
    arrive(PH_SB1, bm_s1, br_s1)
    bias_table(br_s1, 4, bt_t, False)
    y = tri_attend(x, wso_t[0])
    swap_pair(y, 0)
    exchange(PH_Z1, lambda p: z_block(0, p), rz.at[0])
    bias_message(ln(y), web[0], 4, bm_e1)
    exchange(PH_EB1, lambda p: bm_e1, br_e1)
    far_forward(PH_C2, 1)
    exchange(PH_M2, lambda p: sm2.at[p], rm2)
    arrive(PH_Z1, z_block(0, 0), rz.at[0])
    take_pair(0)
    x = z_features()
    tri_project(ln(x), wei[0])
    arrive(PH_EB1, bm_e1, br_e1)
    bias_table(br_e1, 4, bt_t, True)
    y = tri_attend(x, weo_t[0])
    bias_message(ln(y), wrb[1], N, bm_r2)
    exchange(PH_RB2, lambda p: bm_r2, br_r2)
    for t in range(4):
        zst[W * t:W * t + W, :] = jnp.transpose(y[:, W * t:W * t + W]).astype(BF16)

    far_arrive(PH_C2, 1)
    opm(1)
    x = z_features()
    xln = ln(x)
    bias_message(xln, web[1], 4, bm_e2)
    exchange(PH_EB2, lambda p: bm_e2, br_e2)
    tri_project(xln, wei[1])

    arrive(PH_M2, sm2.at[0], rm2)
    rowf[...] = rm2[...].reshape(1024, W).astype(F32)

    def load2(pair):
        xt = jnp.transpose(rowf[pl.ds(pair, R, stride=16), :])
        return jnp.concatenate([xt[0:R], xt[R:W]], axis=1)

    def store2(pair, yt):
        mo_ref[pair] = yt[0:R].astype(BF16)
        mo_ref[pair + 16] = yt[R:W].astype(BF16)

    row_project(1, load2)
    arrive(PH_RB2, bm_r2, br_r2)
    bias_table(br_r2, N, bt_r, True)
    row_loop(0, 2)

    arrive(PH_EB2, bm_e2, br_e2)
    bias_table(br_e2, 4, bt_t, False)
    y = tri_attend(x, weo_t[1])
    swap_pair(y, 1)
    exchange(PH_Z2, lambda p: z_block(1, p), rz.at[1])
    bias_message(ln(y), wsb[1], 4, bm_s2)
    exchange(PH_SB2, lambda p: bm_s2, br_s2)
    row_loop(2, 4)
    row_finish(1, store2)
    arrive(PH_Z2, z_block(1, 0), rz.at[1])
    take_pair(1)
    x = z_features()
    tri_project(ln(x), wsi[1])
    arrive(PH_SB2, bm_s2, br_s2)
    bias_table(br_s2, 4, bt_t, True)
    y = tri_attend(x, wso_t[1])
    for t in range(4):
        zo_ref[2 * t:2 * t + 2] = jnp.transpose(y[:, W * t:W * t + W]).astype(BF16).reshape(2, R, W)

    for c in started:
        c().wait_send()


def solution(mesh):
    axis = 'dap'

    def local_step(m, z, msa_mask, res_mask, w_row_bias, w_row_in, w_row_out, w_col_in, w_col_out, w_opm_in, w_opm_out,
                   w_ts_bias, w_ts_in, w_ts_out, w_te_bias, w_te_in, w_te_out):
        def tin(w):
            return jnp.moveaxis(w, 1, -1).reshape(2, -1, w.shape[1])

        args = (m, z, msa_mask.T, res_mask[None, :],
                tin(w_row_bias), tin(w_row_in), w_row_out.reshape(2, R, R), tin(w_col_in), w_col_out.reshape(2, R, R),
                tin(w_opm_in), w_opm_out.reshape(2, 1024, W),
                tin(w_ts_bias), tin(w_ts_in), w_ts_out.reshape(2, W, W),
                tin(w_te_bias), tin(w_te_in), w_te_out.reshape(2, W, W))
        v = pltpu.VMEM
        scratch = [
            v((N, S), F32), v((R, W), BF16), v((N, R, W), F32), v((R, W), F32),
            v((T, W), BF16), v((W, T), BF16), v((S, S), BF16), v((S, S), BF16),
            v((2, R, R), BF16), v((2, R, R), BF16), v((2, W, W), BF16), v((2, W, W), BF16),
            v((2, S, T), BF16), v((1024, W), F32),
            v((1024, W), F32), v((N, N, 16, W), BF16), v((N, N, 16, W), BF16), v((N, R, S), BF16),
            v((N, N, 16, W), BF16), v((N, N, 16, W), BF16),
            v((2, S, S), BF16), v((2, S, W), F32), v((2, S, S), BF16), v((2, N, S, S), BF16), v((N, S, S), BF16),
            v((T, W), BF16), v((T, W), F32), v((2, T, W), BF16), v((2, N, R, W), BF16), v((R, W), F32),
            v((Q, W), BF16), v((Q, W), BF16), v((N, Q, W), BF16), v((N, Q, W), BF16),
            v((16, W), BF16), v((16, W), BF16), v((16, W), BF16), v((16, W), BF16),
            v((N, 16, W), BF16), v((N, 16, W), BF16), v((N, 16, W), BF16), v((N, 16, W), BF16),
            v((T, W), F32), v((S, W), F32), v((T, T), F32),
            v((4, T, W), F32), v((4, T, W), BF16), v((16, S, W), F32), v((16, R, W), F32), v((16, R, W), F32), v((N, S, W), BF16), v((4, S, W), F32), v((4, S, W), BF16),
            pltpu.SemaphoreType.DMA((12, N)), pltpu.SemaphoreType.DMA((12, N)),
        ]
        vmem = pl.BlockSpec(memory_space=pltpu.VMEM)
        return pl.pallas_call(
            functools.partial(kernel, axis),
            out_shape=(jax.ShapeDtypeStruct((Q, R, R), BF16), jax.ShapeDtypeStruct((N, R, W), BF16)),
            in_specs=[vmem] * len(args),
            out_specs=(vmem, vmem),
            scratch_shapes=scratch,
            compiler_params=pltpu.CompilerParams(collective_id=0, has_side_effects=True, vmem_limit_bytes=58 * 1024 * 1024),
        )(*args)

    in_specs = (P(('data', 'dap')), P(('data', 'dap')), P('data'), P('data')) + (P(),) * 13
    out_specs = (P(('data', 'dap')), P(('data', 'dap')))
    return jax.shard_map(local_step, mesh=mesh, in_specs=in_specs, out_specs=out_specs, check_vma=False)
```

time: 86.6 us -> 69 us (0.80)
  Pallas kernels: 83.2 us -> 65.6 us
    pallas_call x1, Pallas kernels: 83.2 us -> 65.6 us  [local_step(): pl.pallas_call(functools.partial(kernel, axis), out_shape=(jax.ShapeDtype...]
where the time goes in v2:
time: 69 us; the launch traced here: 68.8 us
  Pallas kernels  65.6 us (95%)
  local copies, waits for them, and re-layouts  2.56 us (4%)
    pallas_call x1, Pallas kernels, local_step(): pl.pallas_call(functools.partial(kernel, axis), out_shape=(jax.ShapeDtype...  65.6 us
    unnamed x4, local copies, waits for them, and re-layouts  2.56 us

profile of v2, /device:TPU:0, one launch (start us, length us, event | category | flops | bytes accessed | tf_op | source)
XLA Modules:
  0.0 68.8 jit_solution(13985880272716128617)
XLA Ops:
  0.6 65.6 %shard_map.176 = (bf16[32,64,64]{2,1,0:T(8,128)(2,1)}, bf16[8,64,128]{2,1,0:T(8,128)(2,1)}) custom-call(bf16[32,64,64]{2,1,0:T(8,128)(2,1)} %m_ref.1, bf16[8,64,128]{2,1,0:T(8,128)(2,1)} %z_ref.1, s32[64,256]{1,0:T(8,128)} %bitcast.30, s32[1,64]{1,0:T(1,128)} %bitcast.39, bf16[2,8,128]{2,1,0:T(8,128)(2,1)} %bitcast.36, bf16[2,256,64]{2,1,0:T(8,128)(2,1)} %bitcast.28, ...), custom_call_target="tpu_custom_call" | custom-call | tf_op jit(solution)/shard_map/pallas_call | solution.py:529
  66.2 0.0 copy-start
  66.3 1.9 %copy.21 = bf16[32,64,64]{2,1,0:T(8,128)(2,1)} copy(bf16[32,64,64]{2,1,0:T(8,128)(2,1)} %get-tuple-element.4) | data formatting | bytes 524288
  68.2 0.0 copy-done
  68.2 0.7 copy.22
Async XLA Ops:
  66.2 1.9 %copy-start = (bf16[8,64,128]{2,1,0:T(8,128)(2,1)S(1)}, bf16[8,64,128]{2,1,0:T(8,128)(2,1)}, u32[]{:S(2)}) copy-start(bf16[8,64,128]{2,1,0:T(8,128)(2,1)} %get-tuple-element.5) | copy-start | bytes 393220

commit v3 on v2

--- a/solution.py
+++ b/solution.py
@@ -15,7 +15,7 @@
 N = 8
 R, W, S, T, Q = 64, 128, 256, 512, 32
 
-PH_RB1, PH_M1, PH_C1, PH_SB1, PH_Z1, PH_EB1, PH_RB2, PH_C2, PH_M2, PH_EB2, PH_Z2, PH_SB2 = range(12)
+PH_RB1, PH_M1, PH_SB1, PH_Z1, PH_EB1, PH_RB2, PH_M2, PH_EB2, PH_Z2, PH_SB2, PH_C = range(11)
 
 
 def mm(a, b):
@@ -79,10 +79,14 @@
     return (o * jax.nn.sigmoid(g)).astype(BF16)
 
 
-def kernel(axis, m_ref, z_ref, mt_ref, r_ref, wrb, wri, wro, wci, wco, woi, woo, wsb, wsi, wso, web, wei, weo, mo_ref, zo_ref,
-           mp, mloc, rn, rkey, hm_r, rm_r, hm_t, rm_t, wro_t, wco_t, wso_t, weo_t, wall, wf,
-           rowf, sm1, rm1, m1, sm2, rm2, aloc, remf, rem, cg, xop, zst, zf, sz, rz, pb,
-           bm_r1, bm_r2, br_r1, br_r2, bm_s1, bm_s2, bm_e1, bm_e2, br_s1, br_s2, br_e1, br_e2, bt_r, bt_t, pq, sbuf, pbuf, pqm, xres, obuf, kaug, stri, ptri, send, recv):
+def kernel(axis, *refs):
+    hbm, refs = refs[:17], refs[17:]
+    (mo_ref, zo_ref), held, (load_sem, *refs) = refs[:2], refs[2:19], refs[19:]
+    m_ref, z_ref, mt_ref, r_ref, wrb, wri, wro, wci, wco, woi, woo, wsb, wsi, wso, web, wei, weo = held
+    (mp, mloc, rn, rkey, hm_r, rm_r, hm_t, rm_t, wro_t, wco_t, wso_t, weo_t, wall, wf,
+     rowf, sm1, rm1, m1, sm2, rm2, aloc, remf, rem, cg, xop, zst, zf, sz, rz, pb,
+     bm_r1, bm_r2, br_r1, br_r2, bm_s1, bm_s2, bm_e1, bm_e2, br_s1, br_s2, br_e1, br_e2,
+     bt_r, bt_t, pq, sbuf, pbuf, pqm, xres, obuf, kaug, stri, ptri, send, recv) = refs
     me = lax.axis_index(axis)
     peers = [lax.rem(me + k, N) for k in range(N)]
     senders = [lax.rem(me + N - k, N) for k in range(N)]
@@ -93,6 +97,13 @@
             device_id={axis: peers[k]}, device_id_type=pl.DeviceIdType.MESH)
 
     started = []
+    loads = {id(held[n]): pltpu.make_async_copy(hbm[n], held[n], load_sem.at[n]) for n in range(17)}
+    for ref in (z_ref, wrb, m_ref, mt_ref, wri, wro, r_ref, wci, wco, woi, woo, wsb, wsi, wso, web, wei, weo):
+        loads[id(ref)].start()
+
+    def need(*wanted):
+        for ref in wanted:
+            loads[id(ref)].wait()
 
     chip, core = me // 2, lax.rem(me, 2)
     mate = me + 1 - 2 * core
@@ -104,24 +115,34 @@
             src_ref=src, dst_ref=dst, send_sem=send.at[ph, n], recv_sem=recv.at[ph, n],
             device_id={axis: device}, device_id_type=pl.DeviceIdType.MESH)
 
-    def far_copy(ph, b, n):
-        to, slot = (2 * chips[n] + core, me) if n < 3 else (mate, me) if n == 3 else (mate, 2 * chips[n - 4] + core)
-        return send_to(ph, n, rem.at[b] if n <= 3 else cg.at[b, slot], cg.at[b, slot], to)
-
-    def far_start(ph, b, ns):
+    def far_ref(ref, half):
+        return ref.at[pl.ds(W * half, W), :]
+
+    def far_copy(b, half, n):
+        ph = PH_C + 2 * b + half
+        if n <= 3:
+            to = 2 * chips[n] + core if n < 3 else mate
+            return send_to(ph, n, far_ref(rem.at[b], half), far_ref(cg.at[b, me], half), to)
+        slot = far_ref(cg.at[b, 2 * chips[n - 4] + core], half)
+        return send_to(ph, n, slot, slot, mate)
+
+    def far_start(b, half, ns):
         for n in ns:
-            far_copy(ph, b, n).start()
-            started.append(functools.partial(far_copy, ph, b, n))
-
-    def far_forward(ph, b):
+            far_copy(b, half, n).start()
+            started.append(functools.partial(far_copy, b, half, n))
+
+    def far_got(b, half, n, device):
+        send_to(PH_C + 2 * b + half, n, far_ref(rem.at[b], half), far_ref(cg.at[b, device], half), mate).wait_recv()
+
+    def far_forward(b, half, ns):
+        for n in ns:
+            far_got(b, half, n, 2 * chips[n] + core)
+            far_start(b, half, (4 + n,))
+
+    def far_arrive(b, half):
+        far_got(b, half, 3, mate)
         for n in range(3):
-            send_to(ph, n, rem.at[b], cg.at[b, 2 * chips[n] + core], mate).wait_recv()
-        far_start(ph, b, (4, 5, 6))
-
-    def far_arrive(ph, b):
-        send_to(ph, 3, rem.at[b], cg.at[b, mate], mate).wait_recv()
-        for n in range(3):
-            send_to(ph, 4 + n, rem.at[b], cg.at[b, 2 * chips[n] + 1 - core], mate).wait_recv()
+            far_got(b, half, 4 + n, 2 * chips[n] + 1 - core)
 
     def exchange(ph, src_of, dst_ref):
         for k in range(1, N):
@@ -174,6 +195,7 @@
         return jnp.concatenate(
             [jnp.transpose(zst[W * t:W * t + W, :].astype(F32)) for t in range(4)], axis=1)
 
+    need(z_ref, wrb)
     zst[...] = z_ref[...].reshape(T, W)
     bias_message(ln(z_features()), wrb[0], N, bm_r1)
     pl.semaphore_wait(barrier, N - 1)
@@ -211,7 +233,6 @@
         for n in range(Q):
             a, b = n // 4, n % 4
             wall[0, Q * a:Q * a + Q, W * b:W * b + W] = wf[pl.ds(n, Q, stride=Q), :].astype(BF16)
-            wall[1, Q * a:Q * a + Q, W * b:W * b + W] = woo[1, Q * n:Q * n + Q, :]
 
     def row_project(b, load):
         for c in range(4):
@@ -260,6 +281,7 @@
             for t in range(4):
                 store(4 * c + t, jnp.transpose(y[:, W * t:W * t + W]))
 
+    need(m_ref, mt_ref, wri, wro)
     row_constants()
     row_project(0, lambda pair: jnp.transpose(jnp.concatenate([m_ref[pair], m_ref[pair + 16]], axis=0).astype(F32)))
     arrive(PH_RB1, bm_r1, br_r1)
@@ -273,6 +295,7 @@
     for i in range(R):
         sm1[i // N, i % N] = rowf[pl.ds(i, 16, stride=R), :].astype(BF16)
     exchange(PH_M1, lambda p: sm1.at[p], rm1)
+    need(r_ref, wci, wco, woi, woo, wsb, wsi, wso, web, wei, weo)
     other_constants()
 
     def both(ref, i, rows=slice(None)):
@@ -325,7 +348,8 @@
         def step(i, carry):
             later = jnp.minimum(i + 1, 7)
             if midway is not None:
-                pl.when(i == 6)(midway)
+                for half in range(2):
+                    pl.when(i == (4, 7)[half])(functools.partial(midway, half))
             for h in range(N):
                 logits(i if h < 6 else later, (h + 2) % N, (h + 2) % 4)
                 probs(h % 4)
@@ -364,7 +388,8 @@
 
     column_stack(0, load1, finish1)
     pack_far(0)
-    far_start(PH_C1, 0, (0, 1, 2, 3))
+    for half in range(2):
+        far_start(0, half, (0, 1, 2, 3))
     cg[0, me] = rem[0]
 
     def finish2(i, y):
@@ -372,11 +397,13 @@
         yt = jnp.transpose(jnp.concatenate([y[:, 0:W], y[:, W:S]], axis=0)).astype(BF16)
         sm2[:, i] = yt.reshape(N, 16, W)
 
-    column_stack(1, lambda i: m1[i].astype(F32), finish2, lambda: far_forward(PH_C1, 0))
+    column_stack(1, lambda i: m1[i].astype(F32), finish2, lambda half: far_forward(0, half, range(3)))
     pack_far(1)
 
     def opm(b):
         for n in range(N):
+            if n % 4 == 0:
+                far_arrive(b, n // 4)
             far = cg[b, :, Q * n:Q * n + Q, :].reshape(S, S)
             o = mm_nt(aloc[b], far).astype(BF16)
             for i in range(N):
@@ -388,18 +415,18 @@
             rows = slice(R * i, R * i + R)
             zst[rows, :] = (zst[rows, :].astype(F32) + u * rn[i]).astype(BF16)
 
-    def tri_project(xln, w_in):
+    def tri_part(n, t):
+        return pq[W * n:W * n + W, W * t:W * t + W]
+
+    def tri_logits(xln, w_in):
         pq[...] = rnd(mm(w_in, xln))
+        for t in range(4):
+            stri[t] = pair_logits(tri_part(0, t), tri_part(1, t), 4, hm_t)
 
     def tri_attend(x, w_out_t):
-        def part(n, t):
-            return pq[W * n:W * n + W, W * t:W * t + W]
-
-        for t in range(4):
-            stri[t] = pair_logits(part(0, t), part(1, t), 4, hm_t)
         for t in range(4):
             pair_probs(stri.at[t], ptri.at[t], 4, Q, bt_t, rkey[...])
-        o = jnp.concatenate([pair_values(part(2, t), ptri.at[t], 4, rm_t) for t in range(4)], axis=1)
+        o = jnp.concatenate([pair_values(tri_part(2, t), ptri.at[t], 4, rm_t) for t in range(4)], axis=1)
         return rnd(x + mm(w_out_t, gate(o, pq[3 * W:4 * W, :])))
 
     def swap_pair(y, n):
@@ -417,16 +444,16 @@
     def z_block(n, p):
         return sz.at[n, pl.ds(pl.multiple_of(R * p, R), R), :]
 
-    far_arrive(PH_C1, 0)
-    far_start(PH_C2, 1, (0, 1, 3))
+    far_start(1, 0, (0, 1, 3))
     cg[1, me] = rem[1]
     opm(0)
     x = z_features()
     xln = ln(x)
     bias_message(xln, wsb[0], 4, bm_s1)
     exchange(PH_SB1, lambda p: bm_s1, br_s1)
-    far_start(PH_C2, 1, (2,))
-    tri_project(xln, wsi[0])
+    far_start(1, 0, (2,))
+    far_start(1, 1, (0, 1, 3))
+    tri_logits(xln, wsi[0])
     arrive(PH_SB1, bm_s1, br_s1)
     bias_table(br_s1, 4, bt_t, False)
     y = tri_attend(x, wso_t[0])
@@ -434,27 +461,31 @@
     exchange(PH_Z1, lambda p: z_block(0, p), rz.at[0])
     bias_message(ln(y), web[0], 4, bm_e1)
     exchange(PH_EB1, lambda p: bm_e1, br_e1)
-    far_forward(PH_C2, 1)
+    far_start(1, 1, (2,))
     exchange(PH_M2, lambda p: sm2.at[p], rm2)
+    far_forward(1, 0, range(3))
+    far_forward(1, 1, range(2))
+    for n in range(Q):
+        wall[1, Q * (n // 4):Q * (n // 4) + Q, W * (n % 4):W * (n % 4) + W] = woo[1, Q * n:Q * n + Q, :]
     arrive(PH_Z1, z_block(0, 0), rz.at[0])
     take_pair(0)
     x = z_features()
-    tri_project(ln(x), wei[0])
+    tri_logits(ln(x), wei[0])
     arrive(PH_EB1, bm_e1, br_e1)
     bias_table(br_e1, 4, bt_t, True)
     y = tri_attend(x, weo_t[0])
+    far_forward(1, 1, (2,))
     bias_message(ln(y), wrb[1], N, bm_r2)
     exchange(PH_RB2, lambda p: bm_r2, br_r2)
     for t in range(4):
         zst[W * t:W * t + W, :] = jnp.transpose(y[:, W * t:W * t + W]).astype(BF16)
 
-    far_arrive(PH_C2, 1)
     opm(1)
     x = z_features()
     xln = ln(x)
     bias_message(xln, web[1], 4, bm_e2)
     exchange(PH_EB2, lambda p: bm_e2, br_e2)
-    tri_project(xln, wei[1])
+    tri_logits(xln, wei[1])
 
     arrive(PH_M2, sm2.at[0], rm2)
     rowf[...] = rm2[...].reshape(1024, W).astype(F32)
@@ -464,8 +495,8 @@
         return jnp.concatenate([xt[0:R], xt[R:W]], axis=1)
 
     def store2(pair, yt):
-        mo_ref[pair] = yt[0:R].astype(BF16)
-        mo_ref[pair + 16] = yt[R:W].astype(BF16)
+        mo_ref[pair] = yt[0:R]
+        mo_ref[pair + 16] = yt[R:W]
 
     row_project(1, load2)
     arrive(PH_RB2, bm_r2, br_r2)
@@ -484,12 +515,12 @@
     arrive(PH_Z2, z_block(1, 0), rz.at[1])
     take_pair(1)
     x = z_features()
-    tri_project(ln(x), wsi[1])
+    tri_logits(ln(x), wsi[1])
     arrive(PH_SB2, bm_s2, br_s2)
     bias_table(br_s2, 4, bt_t, True)
     y = tri_attend(x, wso_t[1])
     for t in range(4):
-        zo_ref[2 * t:2 * t + 2] = jnp.transpose(y[:, W * t:W * t + W]).astype(BF16).reshape(2, R, W)
+        zo_ref[2 * t:2 * t + 2] = jnp.transpose(y[:, W * t:W * t + W]).reshape(2, R, W)
 
     for c in started:
         c().wait_send()
@@ -509,7 +540,8 @@
                 tin(w_ts_bias), tin(w_ts_in), w_ts_out.reshape(2, W, W),
                 tin(w_te_bias), tin(w_te_in), w_te_out.reshape(2, W, W))
         v = pltpu.VMEM
-        scratch = [
+        scratch = [v(a.shape, a.dtype) for a in args] + [
+            pltpu.SemaphoreType.DMA((17,)),
             v((N, S), F32), v((R, W), BF16), v((N, R, W), F32), v((R, W), F32),
             v((T, W), BF16), v((W, T), BF16), v((S, S), BF16), v((S, S), BF16),
             v((2, R, R), BF16), v((2, R, R), BF16), v((2, W, W), BF16), v((2, W, W), BF16),
@@ -523,17 +555,18 @@
             v((N, 16, W), BF16), v((N, 16, W), BF16), v((N, 16, W), BF16), v((N, 16, W), BF16),
             v((T, W), F32), v((S, W), F32), v((T, T), F32),
             v((4, T, W), F32), v((4, T, W), BF16), v((16, S, W), F32), v((16, R, W), F32), v((16, R, W), F32), v((N, S, W), BF16), v((4, S, W), F32), v((4, S, W), BF16),
-            pltpu.SemaphoreType.DMA((12, N)), pltpu.SemaphoreType.DMA((12, N)),
+            pltpu.SemaphoreType.DMA((15, N)), pltpu.SemaphoreType.DMA((15, N)),
         ]
         vmem = pl.BlockSpec(memory_space=pltpu.VMEM)
-        return pl.pallas_call(
+        mo, zo = pl.pallas_call(
             functools.partial(kernel, axis),
-            out_shape=(jax.ShapeDtypeStruct((Q, R, R), BF16), jax.ShapeDtypeStruct((N, R, W), BF16)),
-            in_specs=[vmem] * len(args),
+            out_shape=(jax.ShapeDtypeStruct((Q, R, R), F32), jax.ShapeDtypeStruct((N, R, W), F32)),
+            in_specs=[pl.BlockSpec(memory_space=pltpu.HBM)] * len(args),
             out_specs=(vmem, vmem),
             scratch_shapes=scratch,
-            compiler_params=pltpu.CompilerParams(collective_id=0, has_side_effects=True, vmem_limit_bytes=58 * 1024 * 1024),
+            compiler_params=pltpu.CompilerParams(collective_id=0, has_side_effects=True, vmem_limit_bytes=60 * 1024 * 1024),
         )(*args)
+        return mo.astype(BF16), zo.astype(BF16)
 
     in_specs = (P(('data', 'dap')), P(('data', 'dap')), P('data'), P('data')) + (P(),) * 13
     out_specs = (P(('data', 'dap')), P(('data', 'dap')))

time: 69 us -> 67.5 us (0.978)
  other arithmetic: 0 us -> 2.82 us
  local copies, waits for them, and re-layouts: 2.56 us -> 0.01 us
  Pallas kernels: 65.6 us -> 63.9 us
    convert_element_type x0 -> x2, other arithmetic: none -> 2.82 us  [local_step(): return (mo.astype(BF16), zo.astype(BF16))]
    unnamed x4 -> x2, local copies, waits for them, and re-layouts: 2.56 us -> 0.01 us
    pallas_call x1, Pallas kernels: 65.6 us -> 63.9 us  [local_step(): pl.pallas_call(functools.partial(kernel, axis), out_shape=(jax.ShapeDtype...]
where the time goes in v3:
time: 67.5 us; the launch traced here: 67.4 us
  Pallas kernels  63.9 us (95%)
  other arithmetic  2.82 us (4%)
    pallas_call x1, Pallas kernels, local_step(): pl.pallas_call(functools.partial(kernel, axis), out_shape=(jax.ShapeDtype...  63.9 us
    convert_element_type x2, other arithmetic, local_step(): return (mo.astype(BF16), zo.astype(BF16))  2.82 us

profile of v3, /device:TPU:0, one launch (start us, length us, event | category | flops | bytes accessed | tf_op | source)
XLA Modules:
  0.0 67.4 jit_solution(13397463716966633992)
XLA Ops:
  0.6 63.9 %shard_map.176 = (f32[32,64,64]{2,1,0:T(8,128)}, f32[8,64,128]{2,1,0:T(8,128)}) custom-call(bf16[32,64,64]{2,1,0:T(8,128)(2,1)} %refs_0_.1, bf16[8,64,128]{2,1,0:T(8,128)(2,1)} %refs_1_.1, s32[64,256]{1,0:T(8,128)} %bitcast.30, s32[1,64]{1,0:T(1,128)} %bitcast.39, bf16[2,8,128]{2,1,0:T(8,128)(2,1)} %bitcast.36, bf16[2,256,64]{2,1,0:T(8,128)(2,1)} %bitcast.28, ...), custom_call_target="tpu_custom_call" | custom-call | tf_op jit(solution)/shard_map/pallas_call | solution.py:561
  64.5 0.0 copy-start
  64.5 2.1 %convert_element_type.6 = bf16[32,64,64]{2,1,0:T(8,128)(2,1)} convert(f32[32,64,64]{2,1,0:T(8,128)} %get-tuple-element.4) | non-fusion elementwise | flops 131072 | bytes 786432 | tf_op jit(solution)/shard_map/convert_element_type | solution.py:569
  66.7 0.0 copy-done
  66.7 0.7 %convert_element_type.7 = bf16[8,64,128]{2,1,0:T(8,128)(2,1)} convert(f32[8,64,128]{2,1,0:T(8,128)S(1)} %copy-done) | non-fusion elementwise | flops 65536 | bytes 393216 | tf_op jit(solution)/shard_map/convert_element_type | solution.py:569
Async XLA Ops:
  64.5 2.2 %copy-start = (f32[8,64,128]{2,1,0:T(8,128)S(1)}, f32[8,64,128]{2,1,0:T(8,128)}, u32[]{:S(2)}) copy-start(f32[8,64,128]{2,1,0:T(8,128)} %get-tuple-element.5) | copy-start | bytes 786436

commit v4 on v3

--- a/solution.py
+++ b/solution.py
@@ -13,9 +13,10 @@
 NEG = -1e9
 NEG_PARTS = (-2835349504.0, 6914048.0, 8320.0)
 N = 8
-R, W, S, T, Q = 64, 128, 256, 512, 32
-
-PH_RB1, PH_M1, PH_SB1, PH_Z1, PH_EB1, PH_RB2, PH_M2, PH_EB2, PH_Z2, PH_SB2, PH_C = range(11)
+R, W, S, T, Q, H = 64, 128, 256, 512, 32, 16
+TWO, FOUR = range(2), range(4)
+
+PH_RB1, PH_SB1, PH_Z1, PH_EB1, PH_RB2, PH_M2, PH_EB2, PH_Z2, PH_SB2, PH_M1, PH_M1B, PH_C = range(12)
 
 
 def mm(a, b):
@@ -39,6 +40,10 @@
 
 def rnd(x):
     return x.astype(BF16).astype(F32)
+
+
+def flag(x):
+    return jnp.where(x, 1.0, 0.0)
 
 
 def low_lanes(rows):
@@ -86,7 +91,7 @@
     (mp, mloc, rn, rkey, hm_r, rm_r, hm_t, rm_t, wro_t, wco_t, wso_t, weo_t, wall, wf,
      rowf, sm1, rm1, m1, sm2, rm2, aloc, remf, rem, cg, xop, zst, zf, sz, rz, pb,
      bm_r1, bm_r2, br_r1, br_r2, bm_s1, bm_s2, bm_e1, bm_e2, br_s1, br_s2, br_e1, br_e2,
-     bt_r, bt_t, pq, sbuf, pbuf, pqm, xres, obuf, kaug, stri, ptri, send, recv) = refs
+     bt_r, bt_t, pq, sbuf, pbuf, pqm, xres, obuf, kaug, stri, ptri, mst, send, recv) = refs
     me = lax.axis_index(axis)
     peers = [lax.rem(me + k, N) for k in range(N)]
     senders = [lax.rem(me + N - k, N) for k in range(N)]
@@ -187,13 +192,13 @@
                 table[R * (half + h):R * (half + h) + R, :] = jnp.where(lo, xr, x)
             else:
                 t = jnp.transpose(x)
-                for hp in range(2):
+                for hp in TWO:
                     blk = t[R * hp:R * hp + R]
                     table[R * (half * hp + h):R * (half * hp + h) + R, :] = jnp.concatenate([blk, blk], axis=1)
 
     def z_features():
         return jnp.concatenate(
-            [jnp.transpose(zst[W * t:W * t + W, :].astype(F32)) for t in range(4)], axis=1)
+            [jnp.transpose(zst[W * t:W * t + W, :].astype(F32)) for t in FOUR], axis=1)
 
     need(z_ref, wrb)
     zst[...] = z_ref[...].reshape(T, W)
@@ -202,62 +207,65 @@
     exchange(PH_RB1, lambda p: bm_r1, br_r1)
 
     def fill(ref, fn):
-        ref[...] = jnp.where(fn(iota(ref.shape, 0), iota(ref.shape, 1)), 1.0, 0.0).astype(BF16)
+        ref[...] = flag(fn(iota(ref.shape, 0), iota(ref.shape, 1))).astype(BF16)
 
     def row_constants():
         mt_b = mt_ref[...].astype(F32).astype(BF16)
         sel = (iota((S, W), 0) == Q * me + iota((S, W), 1)) & (iota((S, W), 1) < Q)
-        mloc[...] = mm(mt_b, jnp.where(sel, 1.0, 0.0).astype(BF16)).astype(BF16)
+        mloc[...] = mm(mt_b, flag(sel).astype(BF16)).astype(BF16)
         fill(hm_r, lambda r, c: r // R == (c % R) // N)
         fill(rm_r, lambda r, c: (r % R) // N == c // R)
-        for b in range(2):
+        for b in TWO:
             wro_t[b] = jnp.transpose(wro[b].astype(F32)).astype(BF16)
+
+    def far_place(n):
+        return (n % H) // 2, 2 * (n % 2) + n // H
 
     def other_constants():
         mt_b = mt_ref[...].astype(F32).astype(BF16)
         mrows = mt_ref[pl.ds(pl.multiple_of(N * me, N), N), :].astype(F32)
         t = iota((S, S), 1)
-        perm = iota((S, S), 0) == (t % W) // 16 * Q + t // W * 16 + t % 16
-        mp[...] = mm(mrows.astype(BF16), jnp.where(perm, 1.0, 0.0).astype(BF16))
+        perm = iota((S, S), 0) == (t % R) // N * Q + t // W * H + (t % W) // R * N + t % N
+        mp[...] = mm(mrows.astype(BF16), flag(perm).astype(BF16))
         for i in range(N):
             row = jnp.broadcast_to(mrows[i:i + 1, :], (W, S)).astype(BF16)
             rn[i] = 1.0 / (1e-3 + mm_nt(mt_b, row))
         rkey[...] = jnp.transpose(jnp.broadcast_to(r_ref[...].astype(F32), (W, R)))
         fill(hm_t, lambda r, c: r // R == (c % W) // Q)
         fill(rm_t, lambda r, c: (r % W) // Q == c // R)
-        for b in range(2):
+        for b in TWO:
             wco_t[b] = jnp.transpose(wco[b].astype(F32)).astype(BF16)
             wso_t[b] = jnp.transpose(wso[b].astype(F32)).astype(BF16)
             weo_t[b] = jnp.transpose(weo[b].astype(F32)).astype(BF16)
         wf[...] = woo[0].astype(F32)
         for n in range(Q):
-            a, b = n // 4, n % 4
+            a, b = far_place(n)
             wall[0, Q * a:Q * a + Q, W * b:W * b + W] = wf[pl.ds(n, Q, stride=Q), :].astype(BF16)
 
     def row_project(b, load):
-        for c in range(4):
-            x = jnp.concatenate([load(4 * c + t) for t in range(4)], axis=1)
+        for c in FOUR:
+            x = jnp.concatenate([load(4 * c + t) for t in FOUR], axis=1)
             proj = rnd(mm(wri[b], ln(x)))
-            for t in range(4):
+            for t in FOUR:
                 xres[4 * c + t] = x[:, W * t:W * t + W]
                 pqm[4 * c + t] = proj[:, W * t:W * t + W]
 
     def row_loop(lo, hi):
         r, c = iota((W, W), 0), iota((W, W), 1)
-        cs = jnp.where(c < R, 0, 16)
+        cs = jnp.where(c < R, 0, H)
 
         def logits(pair, slot):
             sbuf[slot] = pair_logits(pqm[pair, 0:R, :], pqm[pair, R:2 * R, :], N, hm_r)
 
         def probs(pair, slot):
-            key_mask = mm(mloc[...], jnp.where(r == cs + pair, 1.0, 0.0).astype(BF16))
+            key_mask = mm(mloc[...], flag(r == cs + pair).astype(BF16))
             pair_probs(sbuf.at[slot], pbuf.at[slot], N, N, bt_r, key_mask)
 
         def values(pair, slot):
             obuf[pair] = pair_values(pqm[pair, 2 * R:3 * R, :], pbuf.at[slot], N, rm_r)
 
         def step(n, carry):
-            for t in range(4):
+            for t in FOUR:
                 p = 4 * n + t
                 logits(jnp.minimum(p + 2, 15), (t + 2) % 4)
                 probs(p, t)
@@ -269,32 +277,34 @@
             logits(0, 0)
             logits(1, 1)
         lax.fori_loop(lo, hi, step, 0)
-        if hi == 4:
-            values(15, 3)
-
-    def row_finish(b, store):
-        for c in range(4):
-            g = jnp.concatenate([pqm[4 * c + t, 3 * R:4 * R, :] for t in range(4)], axis=1)
-            o = jnp.concatenate([obuf[4 * c + t] for t in range(4)], axis=1)
-            x = jnp.concatenate([xres[4 * c + t] for t in range(4)], axis=1)
+        values(4 * hi - 1, 3)
+
+    def row_finish(b, store, chunks):
+        for c in chunks:
+            g = jnp.concatenate([pqm[4 * c + t, 3 * R:4 * R, :] for t in FOUR], axis=1)
+            o = jnp.concatenate([obuf[4 * c + t] for t in FOUR], axis=1)
+            x = jnp.concatenate([xres[4 * c + t] for t in FOUR], axis=1)
             y = rnd(x + mm(wro_t[b], gate(o, g)))
-            for t in range(4):
-                store(4 * c + t, jnp.transpose(y[:, W * t:W * t + W]))
+            for t in FOUR:
+                store(4 * c + t, y[:, W * t:W * t + W])
 
     need(m_ref, mt_ref, wri, wro)
     row_constants()
-    row_project(0, lambda pair: jnp.transpose(jnp.concatenate([m_ref[pair], m_ref[pair + 16]], axis=0).astype(F32)))
+    row_project(0, lambda pair: jnp.transpose(jnp.concatenate([m_ref[pair], m_ref[pair + H]], axis=0).astype(F32)))
     arrive(PH_RB1, bm_r1, br_r1)
     bias_table(br_r1, N, bt_r, False)
-    row_loop(0, 4)
-
-    def store1(pair, yt):
+
+    def store1(pair, y):
+        yt = jnp.transpose(y)
         rowf[R * pair:R * pair + R, :] = jnp.concatenate([yt[0:R], yt[R:W]], axis=1)
 
-    row_finish(0, store1)
-    for i in range(R):
-        sm1[i // N, i % N] = rowf[pl.ds(i, 16, stride=R), :].astype(BF16)
-    exchange(PH_M1, lambda p: sm1.at[p], rm1)
+    for half in TWO:
+        row_loop(2 * half, 2 * half + 2)
+        row_finish(0, store1, (2 * half, 2 * half + 1))
+        for n in range(Q):
+            rows = [rowf[pl.ds(T * half + 2 * n + u, N, stride=R), :] for u in TWO]
+            sm1[half, n // 4, n % 4] = jnp.concatenate(rows, axis=0).astype(BF16)
+        exchange(PH_M1 + half, lambda p: sm1.at[half, p], rm1.at[half])
     need(r_ref, wci, wco, woi, woo, wsb, wsi, wso, web, wei, weo)
     other_constants()
 
@@ -317,10 +327,9 @@
             ka = jnp.concatenate([proj[R:2 * R] * keep, flags * (1.0 - keep)], axis=0)
             kaug[i] = jnp.transpose(ka).astype(BF16)
 
-    def column_stack(b, load, finish, midway=None):
-        column_project(b, load)
+    def column_machine():
         head = iota((R, S), 0) // N
-        ones = jnp.where(iota((R, S), 0) < 3, 1.0, 0.0)
+        ones = flag(iota((R, S), 0) < 3)
 
         def logits(i, h, slot):
             q = jnp.where(head == h, both(pqm, i, slice(0, R)), 0.0)
@@ -329,7 +338,7 @@
             sbuf[slot, S:2 * S, :] = s[:, W:S]
 
         def probs(slot):
-            for n in range(2):
+            for n in TWO:
                 rows = slice(S * n, S * n + S)
                 pbuf[slot, rows, :] = softmax_keys(sbuf[slot, rows, :], N ** -0.5 * LOG2E)
 
@@ -341,77 +350,101 @@
             obuf[2 * i, N * h:N * h + N, :] = o[:, 0:W]
             obuf[2 * i + 1, N * h:N * h + N, :] = o[:, W:S]
 
-        pbuf[3] = jnp.zeros((T, W), BF16)
-        logits(0, 0, 0)
-        logits(0, 1, 1)
-
-        def step(i, carry):
-            later = jnp.minimum(i + 1, 7)
-            if midway is not None:
-                for half in range(2):
-                    pl.when(i == (4, 7)[half])(functools.partial(midway, half))
-            for h in range(N):
-                logits(i if h < 6 else later, (h + 2) % N, (h + 2) % 4)
-                probs(h % 4)
-                values(jnp.maximum(i - 1, 0) if h == 0 else i, (h + 7) % N, (h + 3) % 4)
-            return carry
-
-        lax.fori_loop(0, N, step, 0)
-        values(7, 7, 3)
-        for i in range(N):
+        def begin():
+            pbuf[3] = jnp.zeros((T, W), BF16)
+            logits(0, 0, 0)
+            logits(0, 1, 1)
+
+        def loop(lo, hi, at=None, event=None):
+            def step(i, carry):
+                if event is not None:
+                    pl.when(i == at)(event)
+                later = jnp.minimum(i + 1, 7)
+                for h in range(N):
+                    logits(i if h < 6 else later, (h + 2) % N, (h + 2) % 4)
+                    probs(h % 4)
+                    values(jnp.maximum(i - 1, 0) if h == 0 else i, (h + 7) % N, (h + 3) % 4)
+                return carry
+
+            lax.fori_loop(lo, hi, step, 0)
+
+        return begin, loop, lambda i: values(i, 7, 3)
+
+    column_begin, column_loop, column_drain = column_machine()
+
+    def column_finish(b, half, finish):
+        column_drain(4 * half + 3)
+        for i in range(4 * half, 4 * half + 4):
             y = rnd(both(xres, i) + mm(wco_t[b], gate(both(obuf, i), both(pqm, i, slice(3 * R, 4 * R)))))
             finish(i, y)
+        pack_far(b, half)
 
     def opm_operands(b, xt, i):
         proj = mm(woi[b], ln(xt)) * mp[i:i + 1, :]
         near, far = (proj[0:Q], proj[Q:R]) if b == 0 else (proj[Q:R], proj[0:Q])
         rows = slice(Q * i, Q * i + Q)
         aloc[b, rows, :] = near.astype(BF16)
-        remf[0, rows, :] = far[:, 0:W]
-        remf[1, rows, :] = far[:, W:S]
-
-    def pack_far(b):
-        for n in range(16):
-            for t in range(2):
-                rem[b, 16 * n:16 * n + 16, W * t:W * t + W] = jnp.concatenate(
-                    [remf[t, pl.ds(2 * n + u, N, stride=Q), :] for u in range(2)], axis=0).astype(BF16)
-
-    arrive(PH_M1, sm1.at[0], rm1)
+        for qh in TWO:
+            at = W * (i // 4) + H * (4 * qh + i % 4)
+            for t in TWO:
+                remf[t, at:at + H, :] = far[H * qh:H * qh + H, W * t:W * t + W]
+
+    def pack_far(b, half):
+        for n in range(N):
+            for t in TWO:
+                at = W * half + H * n
+                rem[b, at:at + H, W * t:W * t + W] = jnp.concatenate(
+                    [remf[t, pl.ds(W * half + 2 * n + u, N, stride=H), :] for u in TWO], axis=0).astype(BF16)
+
+    for half in TWO:
+        arrive(PH_M1 + half, sm1.at[half, 0], rm1.at[half])
 
     def load1(i):
-        xt = jnp.transpose(rm1[:, i].reshape(W, W).astype(F32))
+        rows = slice(N * (i % 2), N * (i % 2) + N)
+        xt = jnp.transpose(jnp.concatenate(
+            [rm1[half, :, i // 2].astype(F32)[:, rows, :].reshape(R, W) for half in TWO], axis=0))
         return jnp.concatenate([xt[0:R], xt[R:W]], axis=1)
 
     def finish1(i, y):
         m1[i] = y.astype(BF16)
         opm_operands(0, y, i)
 
-    column_stack(0, load1, finish1)
-    pack_far(0)
-    for half in range(2):
-        far_start(0, half, (0, 1, 2, 3))
+    column_project(0, load1)
+    column_begin()
+    for half in TWO:
+        column_loop(4 * half, 4 * half + 4)
+        column_finish(0, half, finish1)
+        far_start(0, half, FOUR)
     cg[0, me] = rem[0]
 
     def finish2(i, y):
         opm_operands(1, y, i)
-        yt = jnp.transpose(jnp.concatenate([y[:, 0:W], y[:, W:S]], axis=0)).astype(BF16)
-        sm2[:, i] = yt.reshape(N, 16, W)
-
-    column_stack(1, lambda i: m1[i].astype(F32), finish2, lambda half: far_forward(0, half, range(3)))
-    pack_far(1)
+        yt = jnp.transpose(jnp.concatenate([y[:, 0:W], y[:, W:S]], axis=0)).reshape(2, N, N, W)
+        sm2[:, i] = jnp.concatenate([yt[0], yt[1]], axis=1).astype(BF16)
+
+    column_project(1, lambda i: m1[i].astype(F32))
+    column_begin()
+    column_loop(0, 4, 1, lambda: far_forward(0, 0, range(3)))
+    column_finish(1, 0, finish2)
+    far_start(1, 0, FOUR)
+    column_loop(4, 6, 5, lambda: far_forward(0, 1, range(3)))
 
     def opm(b):
+        for half in TWO:
+            far_arrive(b, half)
         for n in range(N):
-            if n % 4 == 0:
-                far_arrive(b, n // 4)
-            far = cg[b, :, Q * n:Q * n + Q, :].reshape(S, S)
+            far = jnp.concatenate(
+                [cg[b, :, W * half + H * n:W * half + H * n + H, :].reshape(W, S) for half in TWO], axis=0)
             o = mm_nt(aloc[b], far).astype(BF16)
             for i in range(N):
                 xop[i, Q * n:Q * n + Q, :] = o[Q * i:Q * i + Q, :]
-
+        first = iota((1, 1, N, W), 2) < 4
         for i in range(N):
-            y = mm(jnp.transpose(xop[i]), wall[b]).reshape(N, 4, N, T)
-            u = sum(y[:, n, :, W * n:W * n + W] for n in range(4)).reshape(R, W)
+            y = mm(jnp.transpose(xop[i]), wall[b]).reshape(2, N, 2, N, T)
+            u = sum(jnp.where(first, y[:, :, n, :, 2 * W * n:2 * W * n + W], y[:, :, n, :, 2 * W * n + W:2 * W * n + 2 * W])
+                    for n in TWO)
+            u = (u.reshape(H, N, W) + pltpu.roll(u.reshape(H, N, W), 4, 1)).reshape(2, N, N, W)
+            u = jnp.where(first[0], u[0], u[1]).reshape(R, W)
             rows = slice(R * i, R * i + R)
             zst[rows, :] = (zst[rows, :].astype(F32) + u * rn[i]).astype(BF16)
 
@@ -420,20 +453,20 @@
 
     def tri_logits(xln, w_in):
         pq[...] = rnd(mm(w_in, xln))
-        for t in range(4):
+        for t in FOUR:
             stri[t] = pair_logits(tri_part(0, t), tri_part(1, t), 4, hm_t)
 
     def tri_attend(x, w_out_t):
-        for t in range(4):
+        for t in FOUR:
             pair_probs(stri.at[t], ptri.at[t], 4, Q, bt_t, rkey[...])
-        o = jnp.concatenate([pair_values(tri_part(2, t), ptri.at[t], 4, rm_t) for t in range(4)], axis=1)
+        o = jnp.concatenate([pair_values(tri_part(2, t), ptri.at[t], 4, rm_t) for t in FOUR], axis=1)
         return rnd(x + mm(w_out_t, gate(o, pq[3 * W:4 * W, :])))
 
     def swap_pair(y, n):
-        for t in range(4):
+        for t in FOUR:
             zf[W * t:W * t + W, :] = jnp.transpose(y[:, W * t:W * t + W])
         for c in range(Q):
-            sz[n, 16 * c:16 * c + 16, :] = jnp.concatenate(
+            sz[n, H * c:H * c + H, :] = jnp.concatenate(
                 [zf[pl.ds(2 * c, N, stride=R), :], zf[pl.ds(2 * c + 1, N, stride=R), :]], axis=0).astype(BF16)
 
     def take_pair(n):
@@ -444,16 +477,16 @@
     def z_block(n, p):
         return sz.at[n, pl.ds(pl.multiple_of(R * p, R), R), :]
 
-    far_start(1, 0, (0, 1, 3))
-    cg[1, me] = rem[1]
     opm(0)
     x = z_features()
     xln = ln(x)
     bias_message(xln, wsb[0], 4, bm_s1)
     exchange(PH_SB1, lambda p: bm_s1, br_s1)
-    far_start(1, 0, (2,))
+    tri_logits(xln, wsi[0])
+    column_loop(6, N)
+    column_finish(1, 1, finish2)
     far_start(1, 1, (0, 1, 3))
-    tri_logits(xln, wsi[0])
+    cg[1, me] = rem[1]
     arrive(PH_SB1, bm_s1, br_s1)
     bias_table(br_s1, 4, bt_t, False)
     y = tri_attend(x, wso_t[0])
@@ -464,9 +497,10 @@
     far_start(1, 1, (2,))
     exchange(PH_M2, lambda p: sm2.at[p], rm2)
     far_forward(1, 0, range(3))
-    far_forward(1, 1, range(2))
+    far_forward(1, 1, TWO)
     for n in range(Q):
-        wall[1, Q * (n // 4):Q * (n // 4) + Q, W * (n % 4):W * (n % 4) + W] = woo[1, Q * n:Q * n + Q, :]
+        a, b = far_place(n)
+        wall[1, Q * a:Q * a + Q, W * b:W * b + W] = woo[1, Q * n:Q * n + Q, :]
     arrive(PH_Z1, z_block(0, 0), rz.at[0])
     take_pair(0)
     x = z_features()
@@ -477,7 +511,7 @@
     far_forward(1, 1, (2,))
     bias_message(ln(y), wrb[1], N, bm_r2)
     exchange(PH_RB2, lambda p: bm_r2, br_r2)
-    for t in range(4):
+    for t in FOUR:
         zst[W * t:W * t + W, :] = jnp.transpose(y[:, W * t:W * t + W]).astype(BF16)
 
     opm(1)
@@ -491,12 +525,11 @@
     rowf[...] = rm2[...].reshape(1024, W).astype(F32)
 
     def load2(pair):
-        xt = jnp.transpose(rowf[pl.ds(pair, R, stride=16), :])
+        xt = jnp.transpose(rowf[pl.ds(pair, R, stride=H), :])
         return jnp.concatenate([xt[0:R], xt[R:W]], axis=1)
 
-    def store2(pair, yt):
-        mo_ref[pair] = yt[0:R]
-        mo_ref[pair + 16] = yt[R:W]
+    def store2(pair, y):
+        mst[pair] = y.astype(BF16)
 
     row_project(1, load2)
     arrive(PH_RB2, bm_r2, br_r2)
@@ -511,7 +544,9 @@
     bias_message(ln(y), wsb[1], 4, bm_s2)
     exchange(PH_SB2, lambda p: bm_s2, br_s2)
     row_loop(2, 4)
-    row_finish(1, store2)
+    row_finish(1, store2, FOUR)
+    m_copy = pltpu.make_async_copy(mst, mo_ref, load_sem.at[17])
+    m_copy.start()
     arrive(PH_Z2, z_block(1, 0), rz.at[1])
     take_pair(1)
     x = z_features()
@@ -519,15 +554,24 @@
     arrive(PH_SB2, bm_s2, br_s2)
     bias_table(br_s2, 4, bt_t, True)
     y = tri_attend(x, wso_t[1])
-    for t in range(4):
-        zo_ref[2 * t:2 * t + 2] = jnp.transpose(y[:, W * t:W * t + W]).reshape(2, R, W)
-
+    for t in FOUR:
+        zo_ref[W * t:W * t + W, :] = jnp.transpose(y[:, W * t:W * t + W]).astype(BF16)
+
+    m_copy.wait()
     for c in started:
         c().wait_send()
 
 
+def unpack(y_ref, z_ref, mo_ref, zo_ref):
+    for pair in range(y_ref.shape[0]):
+        yt = jnp.transpose(y_ref[pair].astype(F32)).astype(BF16)
+        mo_ref[0, pair] = yt[0:R]
+        mo_ref[1, pair] = yt[R:W]
+    zo_ref[...] = z_ref[...].reshape(zo_ref.shape)
+
+
 def solution(mesh):
-    axis = 'dap'
+    axis, steps = 'dap', 4
 
     def local_step(m, z, msa_mask, res_mask, w_row_bias, w_row_in, w_row_out, w_col_in, w_col_out, w_opm_in, w_opm_out,
                    w_ts_bias, w_ts_in, w_ts_out, w_te_bias, w_te_in, w_te_out):
@@ -541,32 +585,40 @@
                 tin(w_te_bias), tin(w_te_in), w_te_out.reshape(2, W, W))
         v = pltpu.VMEM
         scratch = [v(a.shape, a.dtype) for a in args] + [
-            pltpu.SemaphoreType.DMA((17,)),
+            pltpu.SemaphoreType.DMA((18,)),
             v((N, S), F32), v((R, W), BF16), v((N, R, W), F32), v((R, W), F32),
             v((T, W), BF16), v((W, T), BF16), v((S, S), BF16), v((S, S), BF16),
             v((2, R, R), BF16), v((2, R, R), BF16), v((2, W, W), BF16), v((2, W, W), BF16),
             v((2, S, T), BF16), v((1024, W), F32),
-            v((1024, W), F32), v((N, N, 16, W), BF16), v((N, N, 16, W), BF16), v((N, R, S), BF16),
-            v((N, N, 16, W), BF16), v((N, N, 16, W), BF16),
+            v((1024, W), F32), v((2, N, 4, H, W), BF16), v((2, N, 4, H, W), BF16), v((N, R, S), BF16),
+            v((N, N, H, W), BF16), v((N, N, H, W), BF16),
             v((2, S, S), BF16), v((2, S, W), F32), v((2, S, S), BF16), v((2, N, S, S), BF16), v((N, S, S), BF16),
             v((T, W), BF16), v((T, W), F32), v((2, T, W), BF16), v((2, N, R, W), BF16), v((R, W), F32),
             v((Q, W), BF16), v((Q, W), BF16), v((N, Q, W), BF16), v((N, Q, W), BF16),
-            v((16, W), BF16), v((16, W), BF16), v((16, W), BF16), v((16, W), BF16),
-            v((N, 16, W), BF16), v((N, 16, W), BF16), v((N, 16, W), BF16), v((N, 16, W), BF16),
+            v((H, W), BF16), v((H, W), BF16), v((H, W), BF16), v((H, W), BF16),
+            v((N, H, W), BF16), v((N, H, W), BF16), v((N, H, W), BF16), v((N, H, W), BF16),
             v((T, W), F32), v((S, W), F32), v((T, T), F32),
-            v((4, T, W), F32), v((4, T, W), BF16), v((16, S, W), F32), v((16, R, W), F32), v((16, R, W), F32), v((N, S, W), BF16), v((4, S, W), F32), v((4, S, W), BF16),
-            pltpu.SemaphoreType.DMA((15, N)), pltpu.SemaphoreType.DMA((15, N)),
+            v((4, T, W), F32), v((4, T, W), BF16), v((H, S, W), F32), v((H, R, W), F32), v((H, R, W), F32), v((N, S, W), BF16), v((4, S, W), F32), v((4, S, W), BF16), v((H, R, W), BF16),
+            pltpu.SemaphoreType.DMA((H, N)), pltpu.SemaphoreType.DMA((H, N)),
         ]
         vmem = pl.BlockSpec(memory_space=pltpu.VMEM)
         mo, zo = pl.pallas_call(
             functools.partial(kernel, axis),
-            out_shape=(jax.ShapeDtypeStruct((Q, R, R), F32), jax.ShapeDtypeStruct((N, R, W), F32)),
+            out_shape=(jax.ShapeDtypeStruct((H, R, W), BF16), jax.ShapeDtypeStruct((T, W), BF16)),
             in_specs=[pl.BlockSpec(memory_space=pltpu.HBM)] * len(args),
-            out_specs=(vmem, vmem),
+            out_specs=(pl.BlockSpec(memory_space=pltpu.HBM), vmem),
             scratch_shapes=scratch,
             compiler_params=pltpu.CompilerParams(collective_id=0, has_side_effects=True, vmem_limit_bytes=60 * 1024 * 1024),
         )(*args)
-        return mo.astype(BF16), zo.astype(BF16)
+        mo, zo = pl.pallas_call(
+            unpack,
+            grid=(steps,),
+            out_shape=(jax.ShapeDtypeStruct((2, H, R, R), BF16), jax.ShapeDtypeStruct((N, R, W), BF16)),
+            in_specs=[pl.BlockSpec((H // steps, R, W), lambda i: (i, 0, 0)), pl.BlockSpec((T // steps, W), lambda i: (i, 0))],
+            out_specs=(pl.BlockSpec((2, H // steps, R, R), lambda i: (0, i, 0, 0)),
+                       pl.BlockSpec((N // steps, R, W), lambda i: (i, 0, 0))),
+        )(mo, zo)
+        return mo.reshape(Q, R, R), zo
 
     in_specs = (P(('data', 'dap')), P(('data', 'dap')), P('data'), P('data')) + (P(),) * 13
     out_specs = (P(('data', 'dap')), P(('data', 'dap')))

time: 67.5 us -> 63.5 us (0.941)
  other arithmetic: 2.82 us -> 0 us
  Pallas kernels: 63.9 us -> 62.6 us
    pallas_call x1, Pallas kernels: 63.9 us -> 59.4 us  [local_step(): pl.pallas_call(functools.partial(kernel, axis), out_shape=(jax.ShapeDtype...]
    pallas_call x0 -> x1, Pallas kernels: none -> 3.23 us  [local_step(): pl.pallas_call(unpack, grid=(steps,), out_shape=(jax.ShapeDtypeStruct((2,...]
    convert_element_type x2 -> x0, other arithmetic: 2.82 us -> none  [local_step(): return (mo.astype(BF16), zo.astype(BF16))]
where the time goes in v4:
time: 63.5 us; the launch traced here: 63.3 us
  Pallas kernels  62.6 us (99%)
  between operations  0.65 us (1%)
    pallas_call x1, Pallas kernels, local_step(): pl.pallas_call(functools.partial(kernel, axis), out_shape=(jax.ShapeDtype...  59.4 us
    pallas_call x1, Pallas kernels, local_step(): pl.pallas_call(unpack, grid=(steps,), out_shape=(jax.ShapeDtypeStruct((2,...  3.23 us

profile of v4, /device:TPU:0, one launch (start us, length us, event | category | flops | bytes accessed | tf_op | source)
XLA Modules:
  0.0 63.3 jit_solution(5173124733469165454)
XLA Ops:
  0.6 59.4 %shard_map.176 = (bf16[16,64,128]{2,1,0:T(8,128)(2,1)}, bf16[512,128]{1,0:T(8,128)(2,1)}) custom-call(bf16[32,64,64]{2,1,0:T(8,128)(2,1)} %refs_0_.1, bf16[8,64,128]{2,1,0:T(8,128)(2,1)} %refs_1_.1, s32[64,256]{1,0:T(8,128)} %bitcast.31, s32[1,64]{1,0:T(1,128)} %bitcast.40, bf16[2,8,128]{2,1,0:T(8,128)(2,1)} %bitcast.37, bf16[2,256,64]{2,1,0:T(8,128)(2,1)} %bitcast.29, ...), custom_call_target="tpu_custom_call" | custom-call | tf_op jit(solution)/shard_map/pallas_call | solution.py:605
  60.0 3.2 %shard_map.177 = (bf16[2,16,64,64]{3,2,1,0:T(8,128)(2,1)}, bf16[8,64,128]{2,1,0:T(8,128)(2,1)}) custom-call(bf16[16,64,128]{2,1,0:T(8,128)(2,1)} %get-tuple-element.6.y_ref, bf16[512,128]{1,0:T(8,128)(2,1)} %get-tuple-element.7.z_ref), custom_call_target="tpu_custom_call" | custom-call | tf_op jit(solution)/shard_map/pallas_call | solution.py:613
